TPU v7x, 32 devices: a 4x4x1 block of a 4x4x8 slice. The times are simulated.
32 devices in a mesh: dp: 1 (over z), pool: 4 (over y), ep: 8 (over x, core).
Axes of the slice: x: 4, y: 4, z: 1, core: 2. Of those that a mesh axis runs over, the one named last changes fastest.
The devices are a block of a 4x4x8 slice.
Arguments:
- hidden: bfloat16 [4096, 1024], P(('dp', 'pool', 'ep'))
- k_cache: bfloat16 [2, 4096, 128, 1, 128], P(None, ('dp', 'pool', 'ep'))
- v_cache: bfloat16 [2, 4096, 128, 1, 128], P(None, ('dp', 'pool', 'ep'))
- lengths: int32 [4096], P(('dp', 'pool', 'ep'))
- w_query: bfloat16 [2, 1024, 2048], replicated
- w_key: bfloat16 [2, 1024, 128], replicated
- w_value: bfloat16 [2, 1024, 128], replicated
- w_out: bfloat16 [2, 2048, 1024], replicated
- w_router: float32 [2, 1024, 128], replicated
- expert_ids: int32 [2, 4096, 8], P(None, ('dp', 'pool', 'ep'))
- w_gate: bfloat16 [2, 128, 1024, 384], P(None, ('pool', 'ep'))
- w_up: bfloat16 [2, 128, 1024, 384], P(None, ('pool', 'ep'))
- w_down: bfloat16 [2, 128, 384, 1024], P(None, ('pool', 'ep'))
Outputs:
- output: bfloat16 [4096, 1024], P(('dp', 'pool', 'ep'))
All inputs are finite; a program needn't handle non-finite values.
Results may differ from a plain program's by a relative error of at most 0.02.
Values are sent between devices in bfloat16 or wider.
A program may use at most 768 MiB of HBM per device.

v0:
```python
import jax
import jax.numpy as jnp
from jax import lax
from jax.sharding import PartitionSpec as P

EPS = 1e-6
GROUP_AXES = ('pool', 'ep')
BATCH_AXES = ('dp', 'pool', 'ep')


def rms_norm(values):
    wide = values.astype(jnp.float32)
    inv_norm = lax.rsqrt(jnp.mean(wide * wide, axis=-1, keepdims=True) + EPS)
    return (wide * inv_norm).astype(jnp.bfloat16)


def attention_layer(hidden, cache_k, cache_v, lengths, q_weight, k_weight, v_weight, o_weight):
    tok_count, seq_len, kv_heads, head_dim = cache_k.shape
    per_kv = q_weight.shape[1] // (kv_heads * head_dim)
    scale = head_dim ** -0.5
    normed = rms_norm(hidden)
    query = jnp.dot(normed, q_weight, preferred_element_type=jnp.float32).astype(jnp.bfloat16).reshape(tok_count, kv_heads, per_kv, head_dim)
    key_new = jnp.dot(normed, k_weight, preferred_element_type=jnp.float32).astype(jnp.bfloat16).reshape(tok_count, kv_heads, head_dim)
    value_new = jnp.dot(normed, v_weight, preferred_element_type=jnp.float32).astype(jnp.bfloat16).reshape(tok_count, kv_heads, head_dim)
    scores = jnp.einsum('tkgd,tskd->tkgs', query, cache_k, preferred_element_type=jnp.float32) * scale
    valid_pos = jnp.arange(seq_len)[None, :] < lengths[:, None]
    scores = jnp.where(valid_pos[:, None, None, :], scores, -jnp.inf)
    score_new = jnp.einsum('tkgd,tkd->tkg', query, key_new, preferred_element_type=jnp.float32) * scale
    peak_score = jnp.maximum(jnp.max(scores, axis=-1), score_new)
    att_probs = jnp.exp(scores - peak_score[..., None])
    new_prob = jnp.exp(score_new - peak_score)
    norm_total = jnp.sum(att_probs, axis=-1) + new_prob
    att_probs = (att_probs / norm_total[..., None]).astype(jnp.bfloat16)
    new_prob = (new_prob / norm_total).astype(jnp.bfloat16).astype(jnp.float32)
    mixed = jnp.einsum('tkgs,tskd->tkgd', att_probs, cache_v, preferred_element_type=jnp.float32)
    mixed = mixed + new_prob[..., None] * value_new.astype(jnp.float32)[:, :, None, :]
    mixed = mixed.astype(jnp.bfloat16).reshape(tok_count, kv_heads * per_kv * head_dim)
    return (hidden.astype(jnp.float32) + jnp.dot(mixed, o_weight, preferred_element_type=jnp.float32)).astype(jnp.bfloat16)


def route_gates(residual, layer_ids, r_weight):
    routed = rms_norm(residual)
    logits = jnp.dot(routed.astype(jnp.float32), r_weight, preferred_element_type=jnp.float32)
    return routed, jax.nn.softmax(jnp.take_along_axis(logits, layer_ids, axis=1), axis=-1)


def window_slots(keys, groups, capacity):
    count = keys.shape[0]
    sort_order = jnp.argsort(keys, stable=True)
    sorted_keys = keys[sort_order]
    counts = jnp.bincount(keys, length=groups + 1)
    starts = jnp.cumsum(counts) - counts
    ranks = jnp.arange(count, dtype=jnp.int32) - starts[sorted_keys]
    sorted_slot = jnp.where(sorted_keys < groups, sorted_keys * capacity + ranks, groups * capacity)
    slots = jnp.zeros((count,), jnp.int32).at[sort_order].set(sorted_slot)
    item_for_slot = jnp.full((groups * capacity,), count, jnp.int32).at[slots].set(jnp.arange(count, dtype=jnp.int32), mode='drop')
    return slots, item_for_slot


def expert_windows(rows, g_weight, u_weight, d_weight):
    first = jnp.einsum('ecd,edf->ecf', rows, g_weight, preferred_element_type=jnp.float32)
    second = jnp.einsum('ecd,edf->ecf', rows, u_weight, preferred_element_type=jnp.float32)
    inner = (jax.nn.silu(first) * second).astype(jnp.bfloat16)
    return jnp.einsum('ecf,efd->ecd', inner, d_weight, preferred_element_type=jnp.float32).astype(jnp.bfloat16)


def solution(mesh):
    group_size = mesh.shape['pool'] * mesh.shape['ep']

    def device_step(hidden, k_cache, v_cache, lengths, w_query, w_key, w_value, w_out, w_router, expert_ids, w_gate, w_up, w_down):
        tok_count, width = hidden.shape
        layers = expert_ids.shape[0]
        top = expert_ids.shape[2]
        local_experts = w_gate.shape[1]
        link_cap = 2 * tok_count * top // group_size - 1
        expert_cap = group_size * ((link_cap + local_experts - 1) // local_experts)
        for layer in range(layers):
            residual = attention_layer(hidden, k_cache[layer], v_cache[layer], lengths, w_query[layer], w_key[layer], w_value[layer], w_out[layer])
            routed, gates = route_gates(residual, expert_ids[layer], w_router[layer])
            flat_ids = expert_ids[layer].reshape(-1)
            pair_slot, pair_for_slot = window_slots(flat_ids // local_experts, group_size, link_cap)
            send_rows = jnp.take(routed, pair_for_slot // top, axis=0, mode='fill', fill_value=0)
            send_local = jnp.take(flat_ids % local_experts, pair_for_slot, mode='fill', fill_value=local_experts)
            recv_rows = lax.all_to_all(send_rows, GROUP_AXES, 0, 0, tiled=True)
            recv_local = lax.all_to_all(send_local, GROUP_AXES, 0, 0, tiled=True)
            row_slot, row_for_slot = window_slots(recv_local, local_experts, expert_cap)
            expert_in = jnp.take(recv_rows, row_for_slot, axis=0, mode='fill', fill_value=0).reshape(local_experts, expert_cap, width)
            expert_out = expert_windows(expert_in, w_gate[layer], w_up[layer], w_down[layer]).reshape(local_experts * expert_cap, width)
            back_rows = jnp.take(expert_out, row_slot, axis=0, mode='fill', fill_value=0)
            returned = lax.all_to_all(back_rows, GROUP_AXES, 0, 0, tiled=True)
            pair_out = jnp.take(returned, pair_slot, axis=0).reshape(tok_count, top, width)
            combined = jnp.sum(gates[:, :, None] * pair_out.astype(jnp.float32), axis=1)
            hidden = (residual.astype(jnp.float32) + combined).astype(jnp.bfloat16)
        return hidden

    cache_spec = P(None, BATCH_AXES, None, None, None)
    expert_spec = P(None, GROUP_AXES, None, None)
    in_specs = (P(BATCH_AXES, None), cache_spec, cache_spec, P(BATCH_AXES), P(), P(), P(), P(), P(), P(None, BATCH_AXES, None), expert_spec, expert_spec, expert_spec)
    return jax.shard_map(device_step, mesh=mesh, in_specs=in_specs, out_specs=P(BATCH_AXES, None), check_vma=False)
```

profile of v0, /device:TPU:103, one launch (start us, length us, event | category | flops | bytes accessed | tf_op | source)
XLA Modules:
  0.0 602.4 jit_solution(8668094856976830171)
XLA Ops:
  1.0 7.6 %scatter_custom_fusion.6 = s32[33]{0:T(128)S(1)} fusion(s32[1024]{0:T(1024)S(1)} %bitcast.328, s32[1024]{0:T(1024)S(1)} %ne.95, s32[]{:T(128)} %constant.165.clone.1), kind=kCustom, calls=%fused_computation.366 | custom fusion | flops 1024 | bytes 136 | tf_op jit(solution)/shard_map/scatter-add | solution.py:51
  10.4 4.4 sort.64
  14.8 4.5 gather_fusion.2
  19.3 4.4 compare_select_fusion.22
  24.0 16.2 %fusion.139 = s32[1024]{0:T(1024)S(1)} fusion(pred[1024]{0:T(1024)(128)(4,1)S(1)} %get-tuple-element.48, pred[1024]{0:T(1024)(128)(4,1)S(1)} %get-tuple-element.47, pred[1024]{0:T(1024)(128)(4,1)S(1)} %get-tuple-element.46, pred[1024]{0:T(1024)(128)(4,1)S(1)} %get-tuple-element.45, pred[1024]{0:T(1024)(128)(4,1)S(1)} %get-tuple-element.44, ...), kind=kLoop, calls=%fused_computation.322 | loop fusion | flops 31744 | bytes 39016 | tf_op jit(solution)/shard_map/jit(_where)/select_n | solution.py:54
  40.3 4.3 scatter_custom_fusion.7
  45.2 4.3 scatter_custom_fusion.8
  49.5 8.6 %gather_fusion.12 = s32[2016]{0:T(1024)S(1)} fusion(s32[1024]{0:T(1024)S(1)} %get-tuple-element.93, s32[2048]{0:T(1024)S(1)} %pad_clamp_fusion.3), kind=kCustom, calls=%fused_computation.8.clone | custom fusion | bytes 24192 | tf_op jit(solution)/shard_map/jit(_take)/gather | solution.py:83
  58.9 8.0 %all-to-all-start.4 = ((s32[32,63,1]{1,2,0:T(1,128)}), s32[32,63,1]{1,2,0:T(1,128)S(1)}, u32[]{:S(2)}, u32[]{:S(2)}) async-start(s32[32,63,1]{1,2,0:T(1,128)} %bitcast.118), calls=%async_computation.4 | async-start | bytes 32768 | tf_op jit(solution)/shard_map/all_to_all | solution.py:85
  67.2 7.6 %scatter_custom_fusion = s32[33]{0:T(128)S(1)} fusion(s32[1024]{0:T(1024)S(1)} %bitcast.329, s32[1024]{0:T(1024)S(1)} %ne.95, s32[]{:T(128)} %constant.165.clone.1), kind=kCustom, calls=%fused_computation.368 | custom fusion | flops 1024 | bytes 136 | tf_op jit(solution)/shard_map/scatter-add | solution.py:51
  76.6 4.4 sort.62
  80.9 4.5 gather_fusion
  85.5 4.5 compare_select_fusion.28
  90.2 16.2 %fusion.141 = s32[1024]{0:T(1024)S(1)} fusion(pred[1024]{0:T(1024)(128)(4,1)S(1)} %get-tuple-element.74, pred[1024]{0:T(1024)(128)(4,1)S(1)} %get-tuple-element.73, pred[1024]{0:T(1024)(128)(4,1)S(1)} %get-tuple-element.72, pred[1024]{0:T(1024)(128)(4,1)S(1)} %get-tuple-element.71, pred[1024]{0:T(1024)(128)(4,1)S(1)} %get-tuple-element.70, ...), kind=kLoop, calls=%fused_computation.325 | loop fusion | flops 31744 | bytes 39016 | tf_op jit(solution)/shard_map/jit(_where)/select_n | solution.py:54
  106.5 4.3 scatter_custom_fusion.1
  110.8 4.5 scatter_custom_fusion.2
  115.7 8.6 %gather_fusion.6 = s32[2016]{0:T(1024)S(1)} fusion(s32[1024]{0:T(1024)S(1)} %get-tuple-element.99, s32[2048]{0:T(1024)S(1)} %pad_clamp_fusion.7), kind=kCustom, calls=%fused_computation.2.clone | custom fusion | bytes 24192 | tf_op jit(solution)/shard_map/jit(_take)/gather | solution.py:83
  124.9 3.1 fusion.63
  128.6 4.9 fusion.189
  137.7 9.6 %gather_fusion.5 = bf16[2016,1024]{1,0:T(8,128)(2,1)} fusion(bf16[128,1024]{1,0:T(8,128)(2,1)S(1)} %multiply_convert_fusion.3, s32[2048]{0:T(1024)S(1)} %pad_clamp_fusion.5), kind=kCustom, calls=%fused_computation.1.clone | custom fusion | bytes 8265600 | tf_op jit(solution)/shard_map/jit(_take)/gather | solution.py:82
  147.3 6.3 %all-to-all-start.1 = ((s32[32,63,1]{1,2,0:T(1,128)}), s32[32,63,1]{1,2,0:T(1,128)S(1)}, u32[]{:S(2)}, u32[]{:S(2)}) async-start(s32[32,63,1]{1,2,0:T(1,128)} %bitcast.51), calls=%async_computation.1 | async-start | bytes 32768 | tf_op jit(solution)/shard_map/all_to_all | solution.py:85
  153.6 4.1 broadcast_select_fusion.5
  157.7 5.2 all_to_all.48
  162.9 6.3 %all-to-all-start = ((bf16[32,63,1024]{2,1,0:T(8,128)(2,1)}), bf16[32,63,1024]{2,1,0:T(8,128)(2,1)}, u32[]{:S(2)}, u32[]{:S(2)}) async-start(bf16[32,63,1024]{2,1,0:T(8,128)(2,1)} %all_to_all.48), calls=%async_computation | async-start | bytes 8388608 | tf_op jit(solution)/shard_map/all_to_all | solution.py:84
  170.6 14.6 %scatter_custom_fusion.3 = s32[5]{0:T(128)S(1)} fusion(s32[2016]{0:T(1024)S(1)} %reshape.859, s32[2016]{0:T(1024)S(1)} %ne.101, s32[]{:T(128)} %constant.165.clone.1), kind=kCustom, calls=%fused_computation.364 | custom fusion | flops 2016 | bytes 24 | tf_op jit(solution)/shard_map/scatter-add | solution.py:51
  185.4 5.1 sort.63
  190.6 11.8 %gather_fusion.1 = s32[2016]{0:T(1024)S(1)} fusion(s32[2016]{0:T(1024)S(1)} %all_to_all.53, s32[2048]{0:T(1024)S(1)} %pad_clamp_fusion.6), kind=kCustom, calls=%fused_computation.13 | custom fusion | bytes 24192 | tf_op jit(solution)/shard_map/gather | solution.py:50
  206.0 10.3 %scatter_custom_fusion.4 = s32[2016]{0:T(1024)S(1)} fusion(s32[2016]{0:T(1024)S(1)} %compare_select_fusion.21, s32[2016]{0:T(1024)S(1)} %add_select_fusion.5, s32[]{:T(128)} %constant.165.clone.1), kind=kCustom, calls=%fused_computation.334 | custom fusion | bytes 8068 | tf_op jit(solution)/shard_map/scatter | solution.py:55
  216.3 9.9 %scatter_custom_fusion.5 = s32[2048]{0:T(1024)S(1)} fusion(s32[2016]{0:T(1024)S(1)} %compare_select_fusion.17, s32[2016]{0:T(1024)S(1)} %iota.51, s32[]{:T(128)} %constant.173.clone.1), kind=kCustom, calls=%fused_computation.330 | custom fusion | bytes 8196 | tf_op jit(solution)/shard_map/scatter | solution.py:56
  226.4 5.2 all_to_all.50
  231.5 13.7 %gather_fusion.7 = bf16[2048,1024]{1,0:T(8,128)(2,1)} fusion(bf16[2016,1024]{1,0:T(8,128)(2,1)} %all_to_all.50, s32[2048]{0:T(1024)S(1)} %fusion.136), kind=kCustom, calls=%fused_computation.3.clone | custom fusion | bytes 8396800 | tf_op jit(solution)/shard_map/jit(_take)/gather | solution.py:87
  249.7 6.0 fusion.28
  255.7 11.6 %fusion.36 = bf16[4,512,1024]{2,1,0:T(8,128)(2,1)} fusion(bf16[2,4,384,1024]{3,2,1,0:T(8,128)(2,1)} %param.37, f32[4,512,384]{2,1,0:T(8,128)} %fusion.28, bf16[4,512,1024]{2,1,0:T(8,128)(2,1)} %bitcast.309, bf16[2,4,1024,384]{3,2,1,0:T(8,128)(2,1)} %param.36), kind=kOutput, calls=%fused_computation.78 | convolution fusion | flops 3228041216 | bytes 17825792 | tf_op jit(solution)/shard_map/ecf,efd->ecd/dot_general | solution.py:64
  267.3 13.7 %gather_fusion.8 = bf16[2016,1024]{1,0:T(8,128)(2,1)} fusion(bf16[2048,1024]{1,0:T(8,128)(2,1)} %bitcast.304, s32[2048]{0:T(1024)S(1)} %pad_clamp_fusion.4), kind=kCustom, calls=%fused_computation.4.clone | custom fusion | bytes 8265600 | tf_op jit(solution)/shard_map/jit(_take)/gather | solution.py:89
  281.0 4.1 broadcast_select_fusion.4
  285.1 5.2 all_to_all.54
  290.2 6.9 %all-to-all-start.2 = ((bf16[32,63,1024]{2,1,0:T(8,128)(2,1)}), bf16[32,63,1024]{2,1,0:T(8,128)(2,1)}, u32[]{:S(2)}, u32[]{:S(2)}) async-start(bf16[32,63,1024]{2,1,0:T(8,128)(2,1)} %all_to_all.54), calls=%async_computation.2 | async-start | bytes 8388608 | tf_op jit(solution)/shard_map/all_to_all | solution.py:90
  297.5 6.8 %gather_fusion.4 = f32[1024]{0:T(1024)S(1)} fusion(f32[128,128]{1,0:T(8,128)S(1)} %fusion.104, s32[1024]{0:T(1024)S(1)} %reshape.1160), kind=kCustom, calls=%fused_computation.clone | custom fusion | bytes 16384 | tf_op jit(solution)/shard_map/jit(take_along_axis)/gather | solution.py:44
  304.9 48.8 %all-to-all-done.2 = bf16[32,63,1024]{2,1,0:T(8,128)(2,1)} async-done(((bf16[32,63,1024]{2,1,0:T(8,128)(2,1)}), bf16[32,63,1024]{2,1,0:T(8,128)(2,1)}, u32[]{:S(2)}, u32[]{:S(2)}) %all-to-all-start.2) | async-done | bytes 4128800 | tf_op jit(solution)/shard_map/all_to_all | solution.py:90
  353.7 5.2 all_to_all.56
  358.9 7.7 %gather_fusion.9 = bf16[1024,1024]{1,0:T(8,128)(2,1)S(1)} fusion(bf16[2016,1024]{1,0:T(8,128)(2,1)} %all_to_all.56, s32[1024]{0:T(1024)S(1)} %get-tuple-element.97), kind=kCustom, calls=%fused_computation.5.clone | custom fusion | bytes 4198400 | tf_op jit(solution)/shard_map/jit(_take)/gather | solution.py:91
  369.8 3.1 fusion.60
  373.1 4.7 fusion.190
  381.6 9.6 %gather_fusion.11 = bf16[2016,1024]{1,0:T(8,128)(2,1)} fusion(bf16[128,1024]{1,0:T(8,128)(2,1)S(1)} %multiply_convert_fusion.2, s32[2048]{0:T(1024)S(1)} %pad_clamp_fusion.1), kind=kCustom, calls=%fused_computation.7.clone | custom fusion | bytes 8265600 | tf_op jit(solution)/shard_map/jit(_take)/gather | solution.py:82
  391.3 4.0 broadcast_select_fusion.3
  395.3 5.2 all_to_all.57
  400.5 3.8 all-to-all-start.3
  404.4 14.8 %scatter_custom_fusion.9 = s32[5]{0:T(128)S(1)} fusion(s32[2016]{0:T(1024)S(1)} %reshape.907, s32[2016]{0:T(1024)S(1)} %ne.101, s32[]{:T(128)} %constant.165.clone.1), kind=kCustom, calls=%fused_computation.362 | custom fusion | flops 2016 | bytes 24 | tf_op jit(solution)/shard_map/scatter-add | solution.py:51
  419.5 5.1 sort.65
  424.6 11.8 %gather_fusion.3 = s32[2016]{0:T(1024)S(1)} fusion(s32[2016]{0:T(1024)S(1)} %all_to_all.62, s32[2048]{0:T(1024)S(1)} %pad_clamp_fusion.2), kind=kCustom, calls=%fused_computation.15 | custom fusion | bytes 24192 | tf_op jit(solution)/shard_map/gather | solution.py:50
  440.0 9.9 %scatter_custom_fusion.10 = s32[2016]{0:T(1024)S(1)} fusion(s32[2016]{0:T(1024)S(1)} %compare_select_fusion.20, s32[2016]{0:T(1024)S(1)} %add_select_fusion.4, s32[]{:T(128)} %constant.165.clone.1), kind=kCustom, calls=%fused_computation.332 | custom fusion | bytes 8068 | tf_op jit(solution)/shard_map/scatter | solution.py:55
  450.0 9.9 %scatter_custom_fusion.11 = s32[2048]{0:T(1024)S(1)} fusion(s32[2016]{0:T(1024)S(1)} %compare_select_fusion.14, s32[2016]{0:T(1024)S(1)} %iota.57, s32[]{:T(128)} %constant.173.clone.1), kind=kCustom, calls=%fused_computation.328 | custom fusion | bytes 8196 | tf_op jit(solution)/shard_map/scatter | solution.py:56
  460.4 5.2 all_to_all.59
  465.5 13.7 %gather_fusion.13 = bf16[2048,1024]{1,0:T(8,128)(2,1)} fusion(bf16[2016,1024]{1,0:T(8,128)(2,1)} %all_to_all.59, s32[2048]{0:T(1024)S(1)} %fusion.137), kind=kCustom, calls=%fused_computation.9.clone | custom fusion | bytes 8396800 | tf_op jit(solution)/shard_map/jit(_take)/gather | solution.py:87
  483.7 6.0 fusion.22
  489.7 11.5 %fusion.39 = bf16[4,512,1024]{2,1,0:T(8,128)(2,1)} fusion(bf16[2,4,384,1024]{3,2,1,0:T(8,128)(2,1)} %param.37, f32[4,512,384]{2,1,0:T(8,128)} %fusion.22, bf16[4,512,1024]{2,1,0:T(8,128)(2,1)} %bitcast.311, bf16[2,4,1024,384]{3,2,1,0:T(8,128)(2,1)} %param.36), kind=kOutput, calls=%fused_computation.79 | convolution fusion | flops 3228041216 | bytes 17825792 | tf_op jit(solution)/shard_map/ecf,efd->ecd/dot_general | solution.py:64
  501.2 13.7 %gather_fusion.14 = bf16[2016,1024]{1,0:T(8,128)(2,1)} fusion(bf16[2048,1024]{1,0:T(8,128)(2,1)} %bitcast.305, s32[2048]{0:T(1024)S(1)} %pad_clamp_fusion), kind=kCustom, calls=%fused_computation.10.clone | custom fusion | bytes 8265600 | tf_op jit(solution)/shard_map/jit(_take)/gather | solution.py:89
  514.8 4.1 broadcast_select_fusion.2
  518.9 5.2 all_to_all.63
  524.1 6.2 %all-to-all-start.5 = ((bf16[32,63,1024]{2,1,0:T(8,128)(2,1)}), bf16[32,63,1024]{2,1,0:T(8,128)(2,1)}, u32[]{:S(2)}, u32[]{:S(2)}) async-start(bf16[32,63,1024]{2,1,0:T(8,128)(2,1)} %all_to_all.63), calls=%async_computation.5 | async-start | bytes 8388608 | tf_op jit(solution)/shard_map/all_to_all | solution.py:90
  530.7 6.8 %gather_fusion.10 = f32[1024]{0:T(1024)S(1)} fusion(f32[128,128]{1,0:T(8,128)S(1)} %fusion.102, s32[1024]{0:T(1024)S(1)} %reshape.1175), kind=kCustom, calls=%fused_computation.6.clone | custom fusion | bytes 16384 | tf_op jit(solution)/shard_map/jit(take_along_axis)/gather | solution.py:44
  538.0 48.8 %all-to-all-done.5 = bf16[32,63,1024]{2,1,0:T(8,128)(2,1)} async-done(((bf16[32,63,1024]{2,1,0:T(8,128)(2,1)}), bf16[32,63,1024]{2,1,0:T(8,128)(2,1)}, u32[]{:S(2)}, u32[]{:S(2)}) %all-to-all-start.5) | async-done | bytes 4128800 | tf_op jit(solution)/shard_map/all_to_all | solution.py:90
  586.8 5.2 all_to_all.65
  592.0 7.7 %gather_fusion.15 = bf16[1024,1024]{1,0:T(8,128)(2,1)S(1)} fusion(bf16[2016,1024]{1,0:T(8,128)(2,1)} %all_to_all.65, s32[1024]{0:T(1024)S(1)} %copy-done.9), kind=kCustom, calls=%fused_computation.11.clone | custom fusion | bytes 4198400 | tf_op jit(solution)/shard_map/jit(_take)/gather | solution.py:91
  (179 shorter events, 41.8 us)
Async XLA Ops:
  0.8 8.8 %copy-start.2 = (s32[1,128,8]{2,1,0:T(8,128)}, s32[1,128,8]{2,1,0:T(8,128)S(1)}, u32[]{:S(2)}) copy-start(s32[1,128,8]{2,1,0:T(8,128)S(1)} %copy.45) | copy-start | bytes 12292
  44.6 13.5 %copy-start.7 = (s32[1024]{0:T(1024)}, s32[1024]{0:T(1024)S(1)}, u32[]{:S(2)}) copy-start(s32[1024]{0:T(1024)S(1)} %scatter_custom_fusion.7) | copy-start | bytes 12292
  58.1 57.2 %copy-start.6 = (bf16[128,1024]{1,0:T(8,128)(2,1)S(1)}, bf16[128,1024]{1,0:T(8,128)(2,1)}, u32[]{:S(2)}) copy-start(bf16[128,1024]{1,0:T(8,128)(2,1)} %param.25) | copy-start | bytes 786436
  58.2 57.4 %copy-start.10 = (s32[128]{0:T(128)S(1)}, s32[128]{0:T(128)}, u32[]{:S(2)}) copy-start(s32[128]{0:T(128)} %param.28) | copy-start | bytes 1540
  58.9 88.4 %all-to-all-start.4 = ((s32[32,63,1]{1,2,0:T(1,128)}), s32[32,63,1]{1,2,0:T(1,128)S(1)}, u32[]{:S(2)}, u32[]{:S(2)}) async-start(s32[32,63,1]{1,2,0:T(1,128)} %bitcast.118), calls=%async_computation.4 | async-start | bytes 32768 | tf_op jit(solution)/shard_map/all_to_all | solution.py:85
  115.7 8.6 %copy-start.11 = (bf16[2,1024,128]{2,1,0:T(8,128)(2,1)S(1)}, bf16[2,1024,128]{2,1,0:T(8,128)(2,1)}, u32[]{:S(2)}) copy-start(bf16[2,1024,128]{2,1,0:T(8,128)(2,1)} %param.30) | copy-start | bytes 1572868
  115.7 8.9 %copy-start.12 = (bf16[2,1024,128]{2,1,0:T(8,128)(2,1)S(1)}, bf16[2,1024,128]{2,1,0:T(8,128)(2,1)}, u32[]{:S(2)}) copy-start(bf16[2,1024,128]{2,1,0:T(8,128)(2,1)} %param.31) | copy-start | bytes 1572868
  124.6 11.3 %slice-start.4 = ((s8[8388608]{0:T(1024)(128)(4,1)}), s8[4194304]{0:T(1024)(128)(4,1)S(1)}, s32[]{:S(2)}) async-start(s8[8388608]{0:T(1024)(128)(4,1)} %bitcast.338), calls=%async_computation.10 | async-start | bytes 8388608
  124.9 9.3 %slice-start = ((s8[8388608]{0:T(1024)(128)(4,1)}), s8[4194304]{0:T(1024)(128)(4,1)S(1)}, s32[]{:S(2)}) async-start(s8[8388608]{0:T(1024)(128)(4,1)} %bitcast.332), calls=%async_computation.6 | async-start | bytes 8388608
  128.2 6.0 %slice-start.1 = ((s8[8388608]{0:T(1024)(128)(4,1)}), s8[4194304]{0:T(1024)(128)(4,1)S(1)}, s32[]{:S(2)}) async-start(s8[8388608]{0:T(1024)(128)(4,1)} %bitcast.332), calls=%async_computation.7 | async-start | bytes 8388608
  128.6 7.4 %slice-start.5 = ((s8[8388608]{0:T(1024)(128)(4,1)}), s8[4194304]{0:T(1024)(128)(4,1)S(1)}, s32[]{:S(2)}) async-start(s8[8388608]{0:T(1024)(128)(4,1)} %bitcast.338), calls=%async_computation.11 | async-start | bytes 8388608
  147.3 15.6 %all-to-all-start.1 = ((s32[32,63,1]{1,2,0:T(1,128)}), s32[32,63,1]{1,2,0:T(1,128)S(1)}, u32[]{:S(2)}, u32[]{:S(2)}) async-start(s32[32,63,1]{1,2,0:T(1,128)} %bitcast.51), calls=%async_computation.1 | async-start | bytes 32768 | tf_op jit(solution)/shard_map/all_to_all | solution.py:85
  162.9 63.5 %all-to-all-start = ((bf16[32,63,1024]{2,1,0:T(8,128)(2,1)}), bf16[32,63,1024]{2,1,0:T(8,128)(2,1)}, u32[]{:S(2)}, u32[]{:S(2)}) async-start(bf16[32,63,1024]{2,1,0:T(8,128)(2,1)} %all_to_all.48), calls=%async_computation | async-start | bytes 8388608 | tf_op jit(solution)/shard_map/all_to_all | solution.py:84
  247.7 2.0 copy-start
  290.2 7.0 %copy-start.4 = (f32[2,1024,128]{2,1,0:T(8,128)S(1)}, f32[2,1024,128]{2,1,0:T(8,128)}, u32[]{:S(2)}) copy-start(f32[2,1024,128]{2,1,0:T(8,128)} %param.33) | copy-start | bytes 3145732
  290.2 63.5 %all-to-all-start.2 = ((bf16[32,63,1024]{2,1,0:T(8,128)(2,1)}), bf16[32,63,1024]{2,1,0:T(8,128)(2,1)}, u32[]{:S(2)}, u32[]{:S(2)}) async-start(bf16[32,63,1024]{2,1,0:T(8,128)(2,1)} %all_to_all.54), calls=%async_computation.2 | async-start | bytes 8388608 | tf_op jit(solution)/shard_map/all_to_all | solution.py:90
  366.5 14.1 %slice-start.6 = ((s8[8388608]{0:T(1024)(128)(4,1)}), s8[4194304]{0:T(1024)(128)(4,1)S(1)}, s32[]{:S(2)}) async-start(s8[8388608]{0:T(1024)(128)(4,1)} %bitcast.340), calls=%async_computation.12 | async-start | bytes 8388608
  369.8 9.1 %slice-start.2 = ((s8[8388608]{0:T(1024)(128)(4,1)}), s8[4194304]{0:T(1024)(128)(4,1)S(1)}, s32[]{:S(2)}) async-start(s8[8388608]{0:T(1024)(128)(4,1)} %bitcast.335), calls=%async_computation.8 | async-start | bytes 8388608
  373.0 5.9 slice-start.3
  373.1 7.6 %slice-start.7 = ((s8[8388608]{0:T(1024)(128)(4,1)}), s8[4194304]{0:T(1024)(128)(4,1)S(1)}, s32[]{:S(2)}) async-start(s8[8388608]{0:T(1024)(128)(4,1)} %bitcast.340), calls=%async_computation.13 | async-start | bytes 8388608
  400.5 59.9 %all-to-all-start.3 = ((bf16[32,63,1024]{2,1,0:T(8,128)(2,1)}), bf16[32,63,1024]{2,1,0:T(8,128)(2,1)}, u32[]{:S(2)}, u32[]{:S(2)}) async-start(bf16[32,63,1024]{2,1,0:T(8,128)(2,1)} %all_to_all.57), calls=%async_computation.3 | async-start | bytes 8388608 | tf_op jit(solution)/shard_map/all_to_all | solution.py:84
  481.7 2.0 copy-start.1
  524.1 6.2 %copy-start.3 = (s32[1,128,8]{2,1,0:T(8,128)S(1)}, s32[1,128,8]{2,1,0:T(8,128)}, u32[]{:S(2)}) copy-start(s32[1,128,8]{2,1,0:T(8,128)} %copy-done.2) | copy-start | bytes 12292
  524.1 6.3 %copy-start.8 = (s32[1024]{0:T(1024)S(1)}, s32[1024]{0:T(1024)}, u32[]{:S(2)}) copy-start(s32[1024]{0:T(1024)} %copy-done.7) | copy-start | bytes 12292
  524.1 6.3 %copy-start.5 = (f32[2,1024,128]{2,1,0:T(8,128)S(1)}, f32[2,1024,128]{2,1,0:T(8,128)}, u32[]{:S(2)}) copy-start(f32[2,1024,128]{2,1,0:T(8,128)} %param.33) | copy-start | bytes 3145732
  524.1 62.7 %all-to-all-start.5 = ((bf16[32,63,1024]{2,1,0:T(8,128)(2,1)}), bf16[32,63,1024]{2,1,0:T(8,128)(2,1)}, u32[]{:S(2)}, u32[]{:S(2)}) async-start(bf16[32,63,1024]{2,1,0:T(8,128)(2,1)} %all_to_all.63), calls=%async_computation.5 | async-start | bytes 8388608 | tf_op jit(solution)/shard_map/all_to_all | solution.py:90
  538.0 54.0 %copy-start.9 = (s32[1024]{0:T(1024)S(1)}, s32[1024]{0:T(1024)}, u32[]{:S(2)}) copy-start(s32[1024]{0:T(1024)} %get-tuple-element.91) | copy-start | bytes 12292
where the time goes:
time: 612 us; the launch traced here: 602 us
  local copies, waits for them, and re-layouts  264 us (43%)
  other arithmetic  142 us (23%)
  waiting for transfers between devices  98 us (16%)
  matrix products  59.3 us (10%)
  starting transfers between devices  37.5 us (6%)
    all_to_all x2, waiting for transfers between devices, device_step(): returned = lax.all_to_all(back_rows, GROUP_AXES, 0, 0, tiled=True)  97.6 us
    scatter-add x4, other arithmetic, window_slots(): counts = jnp.bincount(keys, length=groups + 1)  44.7 us
    gather x4, local copies, waits for them, and re-layouts, window_slots(): sorted_keys = keys[sort_order]  32.6 us
    select_n x4, other arithmetic, window_slots(): jnp.where(sorted_keys < groups, sorted_keys * capacity + ranks, groups *...  32.5 us
    scatter x4, local copies, waits for them, and re-layouts, window_slots(): slots = jnp.zeros((count,), jnp.int32).at[sort_order].set(sorted_slot)  28.9 us
    scatter x4, local copies, waits for them, and re-layouts, window_slots(): jnp.full((groups * capacity,), count, jnp.int32).at[slots]  28.7 us
    gather x2, local copies, waits for them, and re-layouts, device_step(): jnp.take(expert_out, row_slot, axis=0, mode='fill', fill_value=0)  27.4 us
    gather x2, local copies, waits for them, and re-layouts, device_step(): jnp.take(recv_rows, row_for_slot, axis=0, mode='fill', fill_value=0)  27.4 us
  transfers between devices with their start and end apart: 6, of which 3 were waited for; matrix products, arithmetic and copies ran while one was open for 35% of the time, Pallas kernels for 0%

commit v1 on v0

v1 whole, which is shorter than its diff:
```python
import functools

import jax
import jax.numpy as jnp
from jax import lax
from jax.experimental import pallas as pl
from jax.experimental.pallas import tpu as pltpu
from jax.sharding import PartitionSpec as P

EPS = 1e-6
GROUP_AXES = ('pool', 'ep')
BATCH_AXES = ('dp', 'pool', 'ep')
F32 = jnp.float32
BF16 = jnp.bfloat16
CHUNK = 16
WINDOW = 64
TILE = 256
VMEM_LIMIT = 60 * 1024 * 1024


def rms_norm(wide):
    return (wide * lax.rsqrt(jnp.mean(wide * wide, axis=-1, keepdims=True) + EPS)).astype(BF16)


def dot(a, b):
    return jnp.dot(a, b, preferred_element_type=F32)


def dot_t(a, b):
    return lax.dot_general(a, b, (((1,), (1,)), ((), ())), preferred_element_type=F32)


def split3(w):
    hi = w.astype(BF16)
    rest = w - hi.astype(F32)
    mid = rest.astype(BF16)
    low = (rest - mid.astype(F32)).astype(BF16)
    return hi, mid, low


def attention_kernel(layer, dims, hidden_ref, kc_hbm, vc_hbm, len_ref, wq_hbm, wk_hbm, wv_hbm, wo_hbm, wr_hbm, ids_ref,
                     a_ref, u_ref, gate_ref, slot_ref,
                     kbuf, vbuf, wq, wk, wv, wo, wr, q3, o3, kn3, vn3, ksem, vsem, wsem):
    tok, heads, hd, seq, experts, local, top, blk = dims
    nblk = tok // blk
    w_copies = [pltpu.make_async_copy(src.at[layer], dst, wsem.at[i])
                for i, (src, dst) in enumerate(((wq_hbm, wq), (wk_hbm, wk), (wv_hbm, wv), (wo_hbm, wo), (wr_hbm, wr)))]
    for cp in w_copies[:3]:
        cp.start()

    def kv_copy(b):
        rows = pl.ds(b * blk, blk)
        return (pltpu.make_async_copy(kc_hbm.at[layer, rows], kbuf.at[rows], ksem.at[b]),
                pltpu.make_async_copy(vc_hbm.at[layer, rows], vbuf.at[rows], vsem.at[b]))

    for b in range(nblk):
        kcp, vcp = kv_copy(b)
        kcp.start()
        vcp.start()
    for cp in w_copies[3:]:
        cp.start()

    hidden = hidden_ref[...].astype(F32)
    normed = rms_norm(hidden)
    for cp in w_copies[:3]:
        cp.wait()
    kn3[...] = dot(normed, wk[...]).astype(BF16).astype(F32)
    vn3[...] = dot(normed, wv[...]).astype(BF16).astype(F32)
    for h in range(heads):
        if h % 2 == 0:
            pair = dot(normed, wq[:, h * hd:(h + 2) * hd])
        q3[:, h, :] = pair[:, (h % 2) * hd:(h % 2 + 1) * hd].astype(BF16).astype(F32)

    scale = hd ** -0.5
    lane = lax.broadcasted_iota(jnp.int32, (heads, seq), 1)

    def block(b, carry):
        kcp, vcp = kv_copy(b)
        kcp.wait()
        vcp.wait()
        for j in range(blk):
            t = b * blk + j
            q = q3[t]
            s = dot_t(q.astype(BF16), kbuf[t]) * scale
            s = jnp.where(lane < len_ref[t], s, -jnp.inf)
            sn = jnp.sum(q * kn3[pl.ds(t, 1), :], axis=1, keepdims=True) * scale
            peak = jnp.maximum(jnp.max(s, axis=1, keepdims=True), sn)
            p = jnp.exp(s - peak)
            pn = jnp.exp(sn - peak)
            inv = 1.0 / (jnp.sum(p, axis=1, keepdims=True) + pn)
            pb = (p * inv).astype(BF16)
            pnb = (pn * inv).astype(BF16).astype(F32)
            o = dot(pb, vbuf[t]) + pnb * vn3[pl.ds(t, 1), :]
            o3[t] = o.astype(BF16).astype(F32)
        return carry

    lax.fori_loop(0, nblk, block, 0)

    for cp in w_copies[3:]:
        cp.wait()
    mixed = jnp.concatenate([o3[:, h, :].astype(BF16) for h in range(heads)], axis=1)
    a = (hidden + dot(mixed, wo[...])).astype(BF16)
    a_ref[...] = a
    u = rms_norm(a.astype(F32))
    u_ref[...] = u
    hi, mid, low = split3(wr[...])
    logits = dot(u, hi) + dot(u, mid) + dot(u, low)

    ids = ids_ref[...]
    e_iota = lax.broadcasted_iota(jnp.int32, (tok, experts), 1)
    t_row = lax.broadcasted_iota(jnp.int32, (tok, tok), 0)
    t_col = lax.broadcasted_iota(jnp.int32, (tok, tok), 1)
    before = jnp.where(t_col < t_row, 1.0, 0.0).astype(BF16)
    e_row = lax.broadcasted_iota(jnp.int32, (experts, experts), 0)
    e_col = lax.broadcasted_iota(jnp.int32, (experts, experts), 1)
    same = jnp.where((e_row < e_col) & (e_row // local == e_col // local), 1.0, 0.0).astype(BF16)
    hits = [ids[:, k:k + 1] == e_iota for k in range(top)]
    chosen = hits[0]
    for k in range(1, top):
        chosen = chosen | hits[k]
    chosen = jnp.where(chosen, 1.0, 0.0)
    rank = dot(before, chosen.astype(BF16))
    count = jnp.sum(chosen, axis=0, keepdims=True)
    start = dot(jnp.broadcast_to(count, (8, experts)).astype(BF16), same)[0:1]
    slot_full = rank + start + ((e_iota // local) * WINDOW).astype(F32)
    picked = [jnp.sum(jnp.where(hits[k], logits, 0.0), axis=1, keepdims=True) for k in range(top)]
    peak = picked[0]
    for k in range(1, top):
        peak = jnp.maximum(peak, picked[k])
    ex = [jnp.exp(v - peak) for v in picked]
    total = ex[0]
    for k in range(1, top):
        total = total + ex[k]
    for k in range(top):
        gate_ref[:, k:k + 1] = ex[k] / total
        slot_ref[:, k:k + 1] = jnp.sum(jnp.where(hits[k], slot_full, 0.0), axis=1, keepdims=True).astype(jnp.int32)


def attention(layer, hidden, k_cache, v_cache, lengths, w_query, w_key, w_value, w_out, w_router, ids, local):
    tok, width = hidden.shape
    seq, hd = k_cache.shape[2], k_cache.shape[3]
    heads = w_query.shape[2] // hd
    experts = w_router.shape[2]
    top = ids.shape[1]
    blk = 16
    dims = (tok, heads, hd, seq, experts, local, top, blk)
    vm = pl.BlockSpec(memory_space=pltpu.VMEM)
    hb = pl.BlockSpec(memory_space=pl.ANY)
    sm = pl.BlockSpec(memory_space=pltpu.SMEM)
    return pl.pallas_call(
        functools.partial(attention_kernel, layer, dims),
        out_shape=(jax.ShapeDtypeStruct((tok, width), BF16), jax.ShapeDtypeStruct((tok, width), BF16),
                   jax.ShapeDtypeStruct((tok, top), F32), jax.ShapeDtypeStruct((tok, top), jnp.int32)),
        in_specs=[vm, hb, hb, sm, hb, hb, hb, hb, hb, vm],
        out_specs=(vm, vm, vm, vm),
        scratch_shapes=[
            pltpu.VMEM((tok, seq, hd), BF16), pltpu.VMEM((tok, seq, hd), BF16),
            pltpu.VMEM((width, heads * hd), BF16), pltpu.VMEM((width, hd), BF16), pltpu.VMEM((width, hd), BF16),
            pltpu.VMEM((heads * hd, width), BF16), pltpu.VMEM((width, experts), F32),
            pltpu.VMEM((tok, heads, hd), F32), pltpu.VMEM((tok, heads, hd), F32),
            pltpu.VMEM((tok, hd), F32), pltpu.VMEM((tok, hd), F32),
            pltpu.SemaphoreType.DMA((tok // blk,)), pltpu.SemaphoreType.DMA((tok // blk,)), pltpu.SemaphoreType.DMA((5,)),
        ],
        compiler_params=pltpu.CompilerParams(vmem_limit_bytes=VMEM_LIMIT),
        cost_estimate=pl.CostEstimate(flops=4 * 10 ** 9, bytes_accessed=20 * 10 ** 6, transcendentals=0),
        name='attention',
    )(hidden, k_cache, v_cache, lengths, w_query, w_key, w_value, w_out, w_router, ids)


def tables_kernel(dims, ids_ref, key_ref, cnt_ref):
    layers, group, top, tok, local = dims
    me = lax.axis_index(GROUP_AXES)
    row = lax.broadcasted_iota(jnp.int32, (tok, tok), 0)
    col = lax.broadcasted_iota(jnp.int32, (tok, tok), 1)
    before = jnp.where(row < col, 1.0, 0.0).astype(BF16)
    ones = jnp.ones((8, tok), BF16)
    for layer in range(layers):
        for e in range(local):
            target = me * local + e
            hit = ids_ref[:, layer * top, :] == target
            for k in range(1, top):
                hit = hit | (ids_ref[:, layer * top + k, :] == target)
            hitb = jnp.where(hit, 1.0, 0.0).astype(BF16)
            key_ref[layer * local + e] = jnp.where(hit, dot(hitb, before).astype(jnp.int32), -1024)
            cnt_ref[layer * local + e:layer * local + e + 1, :] = dot_t(ones, hitb)[0:1].astype(jnp.int32)


def tables(ids_all, layers, top, local):
    group, _, tok = ids_all.shape
    vm = pl.BlockSpec(memory_space=pltpu.VMEM)
    return pl.pallas_call(
        functools.partial(tables_kernel, (layers, group, top, tok, local)),
        out_shape=(jax.ShapeDtypeStruct((layers * local, group, tok), jnp.int32),
                   jax.ShapeDtypeStruct((layers * local, group), jnp.int32)),
        in_specs=[vm], out_specs=(vm, vm), name='tables',
    )(ids_all)


def expert_kernel(layer, dims, u_hbm, key_ref, cnt_ref, wg_hbm, wu_hbm, wd_hbm, r_ref,
                  ubuf, xg, xs, ys, yc, wg, wu, wd, tab, usem, wsem):
    pools, tok, local, cap_chunks, pool_chunks = dims
    pool_rows = pool_chunks * CHUNK

    def u_copy(c):
        return pltpu.make_async_copy(u_hbm.at[c], ubuf.at[c], usem.at[c])

    def w_copies(e):
        return [pltpu.make_async_copy(src.at[layer, e], dst.at[e], wsem.at[i, e])
                for i, (src, dst) in enumerate(((wg_hbm, wg), (wu_hbm, wu), (wd_hbm, wd)))]

    for c in range(pools):
        u_copy(c).start()
    for e in range(local):
        for cp in w_copies(e):
            cp.start()

    ys[0] = jnp.zeros(ys.shape[1:], BF16)
    row = lax.broadcasted_iota(jnp.int32, (pool_rows, tok), 0)

    def counts(c):
        even = [cnt_ref[layer * local + e, 2 * c] for e in range(local)]
        odd = [cnt_ref[layer * local + e, 2 * c + 1] for e in range(local)]
        chunks = [(even[e] + odd[e] + (CHUNK - 1)) // CHUNK for e in range(local)]
        return even, odd, chunks

    def gather(c, base):
        u_copy(c).wait()
        even, odd, chunks = counts(c)
        halves = []
        for par in range(2):
            off = jnp.int32(0)
            hit = None
            for e in range(local):
                shift = off * CHUNK + (even[e] if par else 0)
                this = row == key_ref[layer * local + e, pl.ds(2 * c + par, 1), :] + shift
                hit = this if hit is None else hit | this
                off = off + chunks[e]
            halves.append(jnp.where(hit, 1.0, 0.0).astype(BF16))
        pick = jnp.concatenate(halves, axis=1)
        xg[...] = dot(pick, ubuf[c]).astype(BF16).reshape(xg.shape)
        for i in range(pool_chunks):
            tab[c * pool_chunks + i] = 0
        off = jnp.int32(0)
        new_base = []
        for e in range(local):
            def copy(i, carry, e=e, off=off):
                to = e * cap_chunks + base[e] + i
                xs[to] = xg[off + i]
                tab[c * pool_chunks + off + i] = to
                return carry
            lax.fori_loop(0, chunks[e], copy, 0)
            off = off + chunks[e]
            new_base.append(base[e] + chunks[e])
        return tuple(new_base)

    base = lax.fori_loop(0, pools, gather, tuple(jnp.int32(0) for _ in range(local)))

    per = TILE // CHUNK
    for e in range(local):
        for cp in w_copies(e):
            cp.wait()

        def tile(i, carry, e=e):
            at = pl.ds(e * cap_chunks + i * per, per)
            x = xs[at].reshape(TILE, xs.shape[2])
            first = dot(x, wg[e])
            second = dot(x, wu[e])
            inner = (first * (1.0 / (1.0 + jnp.exp(-first))) * second).astype(BF16)
            ys[at] = dot(inner, wd[e]).astype(BF16).reshape(per, CHUNK, xs.shape[2])
            return carry

        lax.fori_loop(0, (base[e] + per - 1) // per, tile, 0)

    jrow = lax.broadcasted_iota(jnp.int32, (WINDOW, pool_rows), 0)
    diff = lax.broadcasted_iota(jnp.int32, (WINDOW, pool_rows), 1) - jrow

    def give_back(c, carry):
        even, odd, chunks = counts(c)
        for i in range(pool_chunks):
            yc[i] = ys[tab[c * pool_chunks + i]]
        halves = []
        for par in range(2):
            off = jnp.int32(0)
            lo = jnp.int32(0)
            hit = None
            for e in range(local):
                n = odd[e] if par else even[e]
                delta = off * CHUNK + (even[e] if par else 0) - lo
                this = (diff == delta) & (jrow >= lo) & (jrow < lo + n)
                hit = this if hit is None else hit | this
                off = off + chunks[e]
                lo = lo + n
            halves.append(jnp.where(hit, 1.0, 0.0).astype(BF16))
        pick = jnp.concatenate(halves, axis=0)
        r_ref[pl.ds(2 * c, 2)] = dot(pick, yc[...].reshape(pool_rows, yc.shape[2])).astype(BF16).reshape(2, WINDOW, yc.shape[2])
        return carry

    lax.fori_loop(0, pools, give_back, 0)


def experts(layer, u_all, keys, cnt, w_gate, w_up, w_down):
    group, tok, width = u_all.shape
    pools = group // 2
    local, ff = w_gate.shape[1], w_gate.shape[3]
    pool_chunks = (2 * (WINDOW - 1) + local * (CHUNK - 1) + CHUNK - 1) // CHUNK
    cap = pl.cdiv(group * CHUNK + pools * (CHUNK - 1), TILE) * TILE
    cap_chunks = cap // CHUNK
    u_pool = u_all.reshape(pools, 2 * tok, width)
    vm = pl.BlockSpec(memory_space=pltpu.VMEM)
    hb = pl.BlockSpec(memory_space=pl.ANY)
    sm = pl.BlockSpec(memory_space=pltpu.SMEM)
    return pl.pallas_call(
        functools.partial(expert_kernel, layer, (pools, tok, local, cap_chunks, pool_chunks)),
        out_shape=jax.ShapeDtypeStruct((group, WINDOW, width), BF16),
        in_specs=[hb, vm, sm, hb, hb, hb],
        out_specs=vm,
        scratch_shapes=[
            pltpu.VMEM((pools, 2 * tok, width), BF16),
            pltpu.VMEM((pool_chunks, CHUNK, width), BF16),
            pltpu.VMEM((local * cap_chunks, CHUNK, width), BF16),
            pltpu.VMEM((local * cap_chunks, CHUNK, width), BF16),
            pltpu.VMEM((pool_chunks, CHUNK, width), BF16),
            pltpu.VMEM((local, width, ff), BF16), pltpu.VMEM((local, width, ff), BF16), pltpu.VMEM((local, ff, width), BF16),
            pltpu.SMEM((pools * pool_chunks,), jnp.int32),
            pltpu.SemaphoreType.DMA((pools,)), pltpu.SemaphoreType.DMA((3, local)),
        ],
        compiler_params=pltpu.CompilerParams(vmem_limit_bytes=VMEM_LIMIT),
        cost_estimate=pl.CostEstimate(flops=6 * 10 ** 9, bytes_accessed=20 * 10 ** 6, transcendentals=0),
        name='experts',
    )(u_pool, keys, cnt, w_gate, w_up, w_down)


def combine_kernel(a_ref, r_ref, gate_ref, slot_ref, x_ref, gmat):
    tok, top = gate_ref.shape
    slots = r_ref.shape[0]
    step = 512
    for j in range(0, slots, step):
        iota = lax.broadcasted_iota(jnp.int32, (tok, step), 1) + j
        g = jnp.zeros((tok, step), F32)
        for k in range(top):
            g = jnp.where(iota == slot_ref[:, k:k + 1], gate_ref[:, k:k + 1], g)
        hi, mid, low = split3(g)
        gmat[0:tok, j:j + step] = hi
        gmat[tok:2 * tok, j:j + step] = mid
        gmat[2 * tok:3 * tok, j:j + step] = low
    width = x_ref.shape[1]
    half = width // 2
    for n in range(0, width, half):
        parts = dot(gmat[...], r_ref[:, n:n + half])
        total = parts[0:tok] + parts[tok:2 * tok] + parts[2 * tok:3 * tok]
        x_ref[:, n:n + half] = (a_ref[:, n:n + half].astype(F32) + total).astype(BF16)


def combine(a, rows, gates, slots):
    tok, width = a.shape
    vm = pl.BlockSpec(memory_space=pltpu.VMEM)
    return pl.pallas_call(
        combine_kernel,
        out_shape=jax.ShapeDtypeStruct((tok, width), BF16),
        in_specs=[vm] * 4, out_specs=vm,
        scratch_shapes=[pltpu.VMEM((3 * tok, rows.shape[0]), BF16)],
        compiler_params=pltpu.CompilerParams(vmem_limit_bytes=VMEM_LIMIT),
        name='combine',
    )(a, rows, gates, slots)


def solution(mesh):
    def device_step(hidden, k_cache, v_cache, lengths, w_query, w_key, w_value, w_out, w_router, expert_ids, w_gate, w_up, w_down):
        tok, width = hidden.shape
        layers, _, top = expert_ids.shape
        local = w_gate.shape[1]
        k_cache = k_cache.reshape(layers, tok, k_cache.shape[2], k_cache.shape[4])
        v_cache = v_cache.reshape(k_cache.shape)
        ids_all = lax.all_gather(jnp.swapaxes(expert_ids, 1, 2).reshape(layers * top, tok), GROUP_AXES, axis=0)
        keys, cnt = tables(ids_all, layers, top, local)
        for layer in range(layers):
            a, u, gates, slots = attention(layer, hidden, k_cache, v_cache, lengths, w_query, w_key, w_value, w_out, w_router, expert_ids[layer], local)
            u_all = lax.all_gather(u, GROUP_AXES, axis=0)
            rows = experts(layer, u_all, keys, cnt, w_gate, w_up, w_down)
            back = lax.all_to_all(rows, GROUP_AXES, 0, 0, tiled=True)
            hidden = combine(a, back.reshape(-1, width), gates, slots)
        return hidden

    cache_spec = P(None, BATCH_AXES, None, None, None)
    expert_spec = P(None, GROUP_AXES, None, None)
    in_specs = (P(BATCH_AXES, None), cache_spec, cache_spec, P(BATCH_AXES), P(), P(), P(), P(), P(), P(None, BATCH_AXES, None), expert_spec, expert_spec, expert_spec)
    return jax.shard_map(device_step, mesh=mesh, in_specs=in_specs, out_specs=P(BATCH_AXES, None), check_vma=False)
```

time: 612 us -> 396 us (0.65)
  the two profiles are of different devices: /device:TPU:103 before, /device:TPU:97 now
where the time goes in v1:
time: 396 us; the launch traced here: 393 us
  Pallas kernels  155 us (39%)
  waiting for transfers between devices  119 us (30%)
  blocking collectives  94.1 us (24%)
  between operations  13.5 us (3%)
  starting transfers between devices  9.08 us (2%)
    pallas_call x2, Pallas kernels, attention(): pl.pallas_call(functools.partial(attention_kernel, layer, dims), out_shap...  102 us
    all_gather x2, waiting for transfers between devices, device_step(): u_all = lax.all_gather(u, GROUP_AXES, axis=0)  67.3 us
    all_to_all x1, blocking collectives, device_step(): back = lax.all_to_all(rows, GROUP_AXES, 0, 0, tiled=True)  61.6 us
    all_to_all x1, waiting for transfers between devices, device_step(): back = lax.all_to_all(rows, GROUP_AXES, 0, 0, tiled=True)  51.4 us
    pallas_call x2, Pallas kernels, experts(): pl.pallas_call(functools.partial(expert_kernel, layer, (pools, tok, local...  39.3 us
    all_gather x1, blocking collectives, device_step(): lax.all_gather(jnp.swapaxes(expert_ids, 1, 2).reshape(layers * top, tok),...  32.5 us
    pallas_call x2, Pallas kernels, combine(): pl.pallas_call(combine_kernel, out_shape=jax.ShapeDtypeStruct((tok, width...  11.6 us
    all_to_all x1, starting transfers between devices, device_step(): back = lax.all_to_all(rows, GROUP_AXES, 0, 0, tiled=True)  9.02 us
  transfers between devices with their start and end apart: 3, of which 3 were waited for; matrix products, arithmetic and copies ran while one was open for 0% of the time, Pallas kernels for 1%

profile of v1, /device:TPU:97, one launch (start us, length us, event | category | flops | bytes accessed | tf_op | source)
XLA Modules:
  0.0 393.2 jit_solution(17656095007397238662)
XLA Ops:
  6.5 0.0 all-gather.5.cloned.1.call-start
  6.6 0.7 fusion
  7.3 0.7 copy.18
  8.0 0.0 copy-start
  8.0 50.8 %attention.2 = (bf16[128,1024]{1,0:T(8,128)(2,1)}, bf16[128,1024]{1,0:T(8,128)(2,1)}, f32[128,8]{1,0:T(8,128)}, s32[128,8]{1,0:T(8,128)}) custom-call(bf16[128,1024]{1,0:T(8,128)(2,1)} %hidden_ref.1, bf16[2,128,128,128]{3,2,1,0:T(8,128)(2,1)} %bitcast.11, bf16[2,128,128,128]{3,2,1,0:T(8,128)(2,1)} %bitcast.13, s32[128]{0:T(128)} %len_ref.3, ...), custom_call_target="tpu_custom_call" | custom-call | flops 4000000000 | bytes 20000000 | tf_op jit(solution)/shard_map/attention/pallas_call | solution.py:150
  58.8 0.1 all-gather.5.cloned.1.call-update
  58.8 0.0 copy-done
  58.9 32.5 %all_gather.17.ids_ref = s32[32,16,128]{2,1,0:T(8,128)} all-gather(s32[1,16,128]{2,1,0:T(8,128)S(1)} %bitcast.20), channel_id=1, replica_groups=mesh['dp'=1,'pool'=4,'ep'=8] {'pool','ep'}, dimensions={0}, use_global_device_ids=true | all-gather | bytes 270336 | tf_op jit(solution)/shard_map/all_gather | solution.py:374
  91.4 3.0 tables.1
  94.3 16.9 %all-gather.5.cloned.1.call-done = bf16[4096,1024]{1,0:T(8,128)(2,1)} async-done(((bf16[128,1024]{1,0:T(8,128)(2,1)}), bf16[4096,1024]{1,0:T(8,128)(2,1)}) %all-gather.5.cloned.1.call-update) | async-done | bytes 8388624 | tf_op jit(solution)/shard_map/all_gather | solution.py:378
  111.2 19.6 %experts.2 = bf16[32,64,1024]{2,1,0:T(8,128)(2,1)} custom-call(bf16[16,256,1024]{2,1,0:T(8,128)(2,1)} %bitcast.16, s32[8,32,128]{2,1,0:T(8,128)} %get-tuple-element.17.key_ref, s32[8,32]{1,0:T(8,128)} %get-tuple-element.18.cnt_ref, bf16[2,4,1024,384]{3,2,1,0:T(8,128)(2,1)} %wg_hbm.3, bf16[2,4,1024,384]{3,2,1,0:T(8,128)(2,1)} %wu_hbm.3, ...), custom_call_target="tpu_custom_call" | custom-call | flops 6000000000 | bytes 20000000 | tf_op jit(solution)/shard_map/experts/pallas_call | solution.py:312
  130.9 9.0 %all-to-all-start = ((bf16[32,64,1024]{2,1,0:T(8,128)(2,1)}), bf16[32,64,1024]{2,1,0:T(8,128)(2,1)}, u32[]{:S(2)}, u32[]{:S(2)}) async-start(bf16[32,64,1024]{2,1,0:T(8,128)(2,1)} %experts.2), calls=%async_computation | async-start | bytes 8388608 | tf_op jit(solution)/shard_map/all_to_all | solution.py:380
  139.9 0.1 all-gather.7.cloned.1.call-start
  140.0 0.7 copy.19
  140.7 51.4 %all-to-all-done = bf16[32,64,1024]{2,1,0:T(8,128)(2,1)} async-done(((bf16[32,64,1024]{2,1,0:T(8,128)(2,1)}), bf16[32,64,1024]{2,1,0:T(8,128)(2,1)}, u32[]{:S(2)}, u32[]{:S(2)}) %all-to-all-start) | async-done | bytes 4194336 | tf_op jit(solution)/shard_map/all_to_all | solution.py:380
  192.1 5.8 %combine.2.hidden_ref = bf16[128,1024]{1,0:T(8,128)(2,1)} custom-call(bf16[128,1024]{1,0:T(8,128)(2,1)} %get-tuple-element.15.a_ref, bf16[2048,1024]{1,0:T(8,128)(2,1)} %bitcast.6.r_ref, f32[128,8]{1,0:T(8,128)} %get-tuple-element.19.gate_ref, s32[128,8]{1,0:T(8,128)} %get-tuple-element.20.slot_ref), custom_call_target="tpu_custom_call" | custom-call | tf_op jit(solution)/shard_map/combine/pallas_call | solution.py:357
  197.9 50.8 %attention.3 = (bf16[128,1024]{1,0:T(8,128)(2,1)}, bf16[128,1024]{1,0:T(8,128)(2,1)}, f32[128,8]{1,0:T(8,128)}, s32[128,8]{1,0:T(8,128)}) custom-call(bf16[128,1024]{1,0:T(8,128)(2,1)} %combine.2.hidden_ref, bf16[2,128,128,128]{3,2,1,0:T(8,128)(2,1)} %bitcast.12, bf16[2,128,128,128]{3,2,1,0:T(8,128)(2,1)} %bitcast.14, s32[128]{0:T(128)} %len_ref.3, ...), custom_call_target="tpu_custom_call" | custom-call | flops 4000000000 | bytes 20000000 | tf_op jit(solution)/shard_map/attention/pallas_call | solution.py:150
  248.7 0.1 all-gather.7.cloned.1.call-update
  248.8 50.4 %all-gather.7.cloned.1.call-done = bf16[4096,1024]{1,0:T(8,128)(2,1)} async-done(((bf16[128,1024]{1,0:T(8,128)(2,1)}), bf16[4096,1024]{1,0:T(8,128)(2,1)}) %all-gather.7.cloned.1.call-update) | async-done | bytes 8388624 | tf_op jit(solution)/shard_map/all_gather | solution.py:378
  299.2 19.7 %experts.3 = bf16[32,64,1024]{2,1,0:T(8,128)(2,1)} custom-call(bf16[16,256,1024]{2,1,0:T(8,128)(2,1)} %bitcast.17, s32[8,32,128]{2,1,0:T(8,128)} %get-tuple-element.17.key_ref, s32[8,32]{1,0:T(8,128)} %get-tuple-element.18.cnt_ref, bf16[2,4,1024,384]{3,2,1,0:T(8,128)(2,1)} %wg_hbm.3, bf16[2,4,1024,384]{3,2,1,0:T(8,128)(2,1)} %wu_hbm.3, ...), custom_call_target="tpu_custom_call" | custom-call | flops 6000000000 | bytes 20000000 | tf_op jit(solution)/shard_map/experts/pallas_call | solution.py:312
  318.9 61.6 %all_to_all.10 = bf16[32,64,1024]{2,1,0:T(8,128)(2,1)} all-to-all(bf16[32,64,1024]{2,1,0:T(8,128)(2,1)} %experts.3), channel_id=1, replica_groups=mesh['dp'=1,'pool'=4,'ep'=8] {'pool','ep'}, dimensions={0} | all-to-all | bytes 8388608 | tf_op jit(solution)/shard_map/all_to_all | solution.py:380
  380.5 5.8 %combine.3 = bf16[128,1024]{1,0:T(8,128)(2,1)} custom-call(bf16[128,1024]{1,0:T(8,128)(2,1)} %get-tuple-element.21.a_ref, bf16[2048,1024]{1,0:T(8,128)(2,1)} %bitcast.15, f32[128,8]{1,0:T(8,128)} %get-tuple-element.23.gate_ref, s32[128,8]{1,0:T(8,128)} %get-tuple-element.24.slot_ref), custom_call_target="tpu_custom_call" | custom-call | tf_op jit(solution)/shard_map/combine/pallas_call | solution.py:357
Async XLA Ops:
  6.5 104.7 %all-gather.5.cloned.1.call-start = ((), (), s32[]{:S(2)}) async-start(), calls=%async_computation.2 | async-start | bytes 8650752 | tf_op jit(solution)/shard_map/all_gather | solution.py:378
  8.0 50.9 %copy-start = (s32[2,128,8]{1,2,0:T(8,128)S(1)}, s32[2,128,8]{1,2,0:T(8,128)}, u32[]{:S(2)}) copy-start(s32[2,128,8]{1,2,0:T(8,128)} %param.22) | copy-start | bytes 24580
  130.9 61.3 %all-to-all-start = ((bf16[32,64,1024]{2,1,0:T(8,128)(2,1)}), bf16[32,64,1024]{2,1,0:T(8,128)(2,1)}, u32[]{:S(2)}, u32[]{:S(2)}) async-start(bf16[32,64,1024]{2,1,0:T(8,128)(2,1)} %experts.2), calls=%async_computation | async-start | bytes 8388608 | tf_op jit(solution)/shard_map/all_to_all | solution.py:380
  139.9 159.3 %all-gather.7.cloned.1.call-start = ((), (), s32[]{:S(2)}) async-start(), calls=%async_computation.3 | async-start | bytes 8650752 | tf_op jit(solution)/shard_map/all_gather | solution.py:378
Sparse Core Ops, SparseCore 0:
  59.0 52.1 all-gather.4
  248.9 50.2 all-gather.6

commit v2 on v1

v2 whole, which is shorter than its diff:
```python
import functools

import jax
import jax.numpy as jnp
from jax import lax
from jax.experimental import pallas as pl
from jax.experimental.pallas import tpu as pltpu
from jax.sharding import PartitionSpec as P

EPS = 1e-6
GROUP_AXES = ('pool', 'ep')
BATCH_AXES = ('dp', 'pool', 'ep')
F32 = jnp.float32
BF16 = jnp.bfloat16
CHUNK = 16
WINDOW = 64
TILE = 256
VMEM_LIMIT = 60 * 1024 * 1024
MESH = pl.DeviceIdType.MESH


def rms_norm(wide):
    return (wide * lax.rsqrt(jnp.mean(wide * wide, axis=-1, keepdims=True) + EPS)).astype(BF16)


def dot(a, b):
    return jnp.dot(a, b, preferred_element_type=F32)


def dot_t(a, b):
    return lax.dot_general(a, b, (((1,), (1,)), ((), ())), preferred_element_type=F32)


def split3(w):
    hi = w.astype(BF16)
    rest = w - hi.astype(F32)
    mid = rest.astype(BF16)
    low = (rest - mid.astype(F32)).astype(BF16)
    return hi, mid, low


def attention_kernel(layer, dims, share, hidden_ref, kc_hbm, vc_hbm, len_ref, wq_hbm, wk_hbm, wv_hbm, wo_hbm, wr_hbm, ids_ref, *refs):
    if share:
        mine_ref, a_ref, u_ref, gs_ref, all_ref, gather_buf, id_send, id_recv, *refs = refs
    else:
        a_ref, u_ref, gs_ref, *refs = refs
    attention_body(layer, dims, hidden_ref, kc_hbm, vc_hbm, len_ref, wq_hbm, wk_hbm, wv_hbm, wo_hbm, wr_hbm, ids_ref, a_ref, u_ref, gs_ref,
                   (lambda: share_ids(share, mine_ref, gather_buf, id_send, id_recv)) if share else None, *refs)
    if share:
        group = share[0] * share[1]
        me = lax.axis_index(GROUP_AXES)
        for d in range(1, group):
            id_copy(share, d, mine_ref, gather_buf, id_send, id_recv).wait()
        gather_buf[me] = mine_ref[...]
        all_ref[...] = gather_buf[...]


def id_copy(share, d, mine_ref, gather_buf, id_send, id_recv):
    pools, eps = share
    me = lax.axis_index(GROUP_AXES)
    to = lax.rem(me + d, pools * eps)
    return pltpu.make_async_remote_copy(
        src_ref=mine_ref, dst_ref=gather_buf.at[me], send_sem=id_send.at[d], recv_sem=id_recv.at[d],
        device_id={'pool': to // eps, 'ep': lax.rem(to, eps)}, device_id_type=MESH)


def share_ids(share, mine_ref, gather_buf, id_send, id_recv):
    pools, eps = share
    group = pools * eps
    me = lax.axis_index(GROUP_AXES)
    barrier = pltpu.get_barrier_semaphore()
    for d in range(1, group):
        to = lax.rem(me + d, group)
        pl.semaphore_signal(barrier, inc=1, device_id={'pool': to // eps, 'ep': lax.rem(to, eps)}, device_id_type=MESH)
    pl.semaphore_wait(barrier, group - 1)
    for d in range(1, group):
        id_copy(share, d, mine_ref, gather_buf, id_send, id_recv).start()


def attention_body(layer, dims, hidden_ref, kc_hbm, vc_hbm, len_ref, wq_hbm, wk_hbm, wv_hbm, wo_hbm, wr_hbm, ids_ref,
                   a_ref, u_ref, gs_ref, after_start,
                   kbuf, vbuf, wq, wk, wv, wo, wr, q3, o3, sbuf, nbuf, kn3, vn3, ksem, vsem, wsem):
    tok, heads, hd, seq, experts, local, top, blk = dims
    nblk = tok // blk
    w_copies = [pltpu.make_async_copy(src.at[layer], dst, wsem.at[i])
                for i, (src, dst) in enumerate(((wq_hbm, wq), (wk_hbm, wk), (wv_hbm, wv), (wo_hbm, wo), (wr_hbm, wr)))]
    for cp in w_copies[:3]:
        cp.start()

    def kv_copy(b):
        rows = pl.ds(b * blk, blk)
        return (pltpu.make_async_copy(kc_hbm.at[layer, rows], kbuf.at[rows], ksem.at[b]),
                pltpu.make_async_copy(vc_hbm.at[layer, rows], vbuf.at[rows], vsem.at[b]))

    for b in range(nblk):
        kcp, vcp = kv_copy(b)
        kcp.start()
        vcp.start()
    for cp in w_copies[3:]:
        cp.start()

    if after_start is not None:
        after_start()
    hidden = hidden_ref[...].astype(F32)
    normed = rms_norm(hidden)
    for cp in w_copies[:3]:
        cp.wait()
    kn3[...] = dot(normed, wk[...]).astype(BF16).astype(F32)
    vn3[...] = dot(normed, wv[...]).astype(BF16).astype(F32)
    for h in range(heads):
        if h % 2 == 0:
            pair = dot(normed, wq[:, h * hd:(h + 2) * hd])
        q3[:, h, :] = pair[:, (h % 2) * hd:(h % 2 + 1) * hd].astype(BF16).astype(F32)

    scale = hd ** -0.5
    lane = lax.broadcasted_iota(jnp.int32, (heads, seq), 1)

    def block(b, carry):
        kcp, vcp = kv_copy(b)
        kcp.wait()
        for j in range(blk):
            t = b * blk + j
            q = q3[t]
            s = dot_t(q.astype(BF16), kbuf[t]) * scale
            sbuf[j * heads:(j + 1) * heads, :] = jnp.where(lane < len_ref[t], s, -jnp.inf)
            nbuf[j * heads:(j + 1) * heads, :] = q * kn3[pl.ds(t, 1), :]
        s = sbuf[...]
        sn = jnp.sum(nbuf[...], axis=1, keepdims=True) * scale
        peak = jnp.maximum(jnp.max(s, axis=1, keepdims=True), sn)
        p = jnp.exp(s - peak)
        pn = jnp.exp(sn - peak)
        inv = 1.0 / (jnp.sum(p, axis=1, keepdims=True) + pn)
        pb = (p * inv).astype(BF16)
        pnb = (pn * inv).astype(BF16).astype(F32)
        vcp.wait()
        for j in range(blk):
            t = b * blk + j
            rows = slice(j * heads, (j + 1) * heads)
            o = dot(pb[rows], vbuf[t]) + pnb[rows] * vn3[pl.ds(t, 1), :]
            o3[t] = o.astype(BF16).astype(F32)
        return carry

    lax.fori_loop(0, nblk, block, 0)

    for cp in w_copies[3:]:
        cp.wait()
    mixed = jnp.concatenate([o3[:, h, :].astype(BF16) for h in range(heads)], axis=1)
    a = (hidden + dot(mixed, wo[...])).astype(BF16)
    a_ref[...] = a
    u = rms_norm(a.astype(F32))
    u_ref[...] = u
    hi, mid, low = split3(wr[...])
    logits = dot(u, hi) + dot(u, mid) + dot(u, low)

    ids = ids_ref[...]
    e_iota = lax.broadcasted_iota(jnp.int32, (tok, experts), 1)
    t_row = lax.broadcasted_iota(jnp.int32, (tok, tok), 0)
    t_col = lax.broadcasted_iota(jnp.int32, (tok, tok), 1)
    before = jnp.where(t_col < t_row, 1.0, 0.0).astype(BF16)
    e_row = lax.broadcasted_iota(jnp.int32, (experts, experts), 0)
    e_col = lax.broadcasted_iota(jnp.int32, (experts, experts), 1)
    same = jnp.where((e_row < e_col) & (e_row // local == e_col // local), 1.0, 0.0).astype(BF16)
    hits = [ids[:, k:k + 1] == e_iota for k in range(top)]
    chosen = hits[0]
    for k in range(1, top):
        chosen = chosen | hits[k]
    chosen = jnp.where(chosen, 1.0, 0.0)
    rank = dot(before, chosen.astype(BF16))
    count = jnp.sum(chosen, axis=0, keepdims=True)
    start = dot(jnp.broadcast_to(count, (8, experts)).astype(BF16), same)[0:1]
    slot_full = rank + start + ((e_iota // local) * WINDOW).astype(F32)
    picked = [jnp.sum(jnp.where(hits[k], logits, 0.0), axis=1, keepdims=True) for k in range(top)]
    peak = picked[0]
    for k in range(1, top):
        peak = jnp.maximum(peak, picked[k])
    ex = [jnp.exp(v - peak) for v in picked]
    total = ex[0]
    for k in range(1, top):
        total = total + ex[k]
    columns = [v / total for v in ex] + [jnp.sum(jnp.where(hit, slot_full, 0.0), axis=1, keepdims=True) for hit in hits]
    columns.append(jnp.zeros((tok, experts - 2 * top), F32))
    gs_ref[...] = jnp.transpose(jnp.concatenate(columns, axis=1))[:2 * top]


def attention(layer, share, hidden, k_cache, v_cache, lengths, w_query, w_key, w_value, w_out, w_router, ids, mine, local):
    tok, width = hidden.shape
    seq, hd = k_cache.shape[2], k_cache.shape[3]
    heads = w_query.shape[2] // hd
    experts = w_router.shape[2]
    top = ids.shape[1]
    blk = 16
    dims = (tok, heads, hd, seq, experts, local, top, blk)
    vm = pl.BlockSpec(memory_space=pltpu.VMEM)
    hb = pl.BlockSpec(memory_space=pl.ANY)
    sm = pl.BlockSpec(memory_space=pltpu.SMEM)
    out_shape = [jax.ShapeDtypeStruct((tok, width), BF16), jax.ShapeDtypeStruct((tok, width), BF16), jax.ShapeDtypeStruct((2 * top, tok), F32)]
    args = [hidden, k_cache, v_cache, lengths, w_query, w_key, w_value, w_out, w_router, ids]
    specs = [vm, hb, hb, sm, hb, hb, hb, hb, hb, vm]
    scratch = []
    params = {}
    if share:
        group = share[0] * share[1]
        args.append(mine)
        specs.append(vm)
        out_shape.append(jax.ShapeDtypeStruct((group,) + mine.shape, mine.dtype))
        scratch = [pltpu.VMEM((group,) + mine.shape, mine.dtype), pltpu.SemaphoreType.DMA((group,)), pltpu.SemaphoreType.DMA((group,))]
        params = dict(collective_id=7, has_side_effects=True)
    return pl.pallas_call(
        functools.partial(attention_kernel, layer, dims, share),
        out_shape=tuple(out_shape),
        in_specs=specs,
        out_specs=tuple(vm for _ in out_shape),
        scratch_shapes=scratch + [
            pltpu.VMEM((tok, seq, hd), BF16), pltpu.VMEM((tok, seq, hd), BF16),
            pltpu.VMEM((width, heads * hd), BF16), pltpu.VMEM((width, hd), BF16), pltpu.VMEM((width, hd), BF16),
            pltpu.VMEM((heads * hd, width), BF16), pltpu.VMEM((width, experts), F32),
            pltpu.VMEM((tok, heads, hd), F32), pltpu.VMEM((tok, heads, hd), F32),
            pltpu.VMEM((blk * heads, seq), F32), pltpu.VMEM((blk * heads, hd), F32),
            pltpu.VMEM((tok, hd), F32), pltpu.VMEM((tok, hd), F32),
            pltpu.SemaphoreType.DMA((tok // blk,)), pltpu.SemaphoreType.DMA((tok // blk,)), pltpu.SemaphoreType.DMA((5,)),
        ],
        compiler_params=pltpu.CompilerParams(vmem_limit_bytes=VMEM_LIMIT, **params),
        cost_estimate=pl.CostEstimate(flops=4 * 10 ** 9, bytes_accessed=20 * 10 ** 6, transcendentals=0),
        name='attention',
    )(*args)


def tables_kernel(dims, ids_ref, key_ref, tab_ref):
    layers, group, top, tok, local, pool_chunks, cap_chunks = dims
    pools = group // 2
    me = lax.axis_index(GROUP_AXES)

    def iota(shape, axis):
        return lax.broadcasted_iota(jnp.int32, shape, axis)

    def onehot(cond):
        return jnp.where(cond, 1.0, 0.0).astype(BF16)

    before_tok = onehot(iota((tok, tok), 0) < iota((tok, tok), 1))
    before_pool = onehot(iota((pools, pools), 1) < iota((pools, pools), 0))
    pair = onehot(iota((pools, group), 1) // 2 == iota((pools, group), 0))
    spread = onehot(iota((group, pools), 0) // 2 == iota((group, pools), 1))
    prev = onehot((iota((group, group), 1) + 1 == iota((group, group), 0)) & (iota((group, group), 0) % 2 == 1))
    lane_p = iota((pools, tok), 1)
    pool_id = iota((pools, tok), 0)
    lane_s = iota((group, tok), 1)

    def to_int(v):
        return v.astype(jnp.int32)

    for layer in range(layers):
        off = jnp.zeros((pools, tok), jnp.int32)
        lo = jnp.zeros((group, tok), jnp.int32)
        tab_y = jnp.zeros((pools, tok), jnp.int32)
        tab_s = jnp.zeros((group, tok), jnp.int32)
        rows_x = []
        for e in range(local):
            target = me * local + e
            hit = ids_ref[:, layer * top, :] == target
            for k in range(1, top):
                hit = hit | (ids_ref[:, layer * top + k, :] == target)
            hitb = onehot(hit)
            rank = to_int(dot(hitb, before_tok))
            count = jnp.broadcast_to(jnp.sum(jnp.where(hit, 1.0, 0.0), axis=1, keepdims=True), (group, tok))
            countb = count.astype(BF16)
            count = to_int(count)
            number = to_int(dot(pair, countb))
            chunks = lax.shift_right_logical(number + (CHUNK - 1), 4)
            base = to_int(dot(before_pool, chunks.astype(F32).astype(BF16)))
            offs = to_int(dot(spread, (off * CHUNK).astype(F32).astype(BF16)))
            shift = offs + to_int(dot(prev, countb))
            key_ref[layer * local + e] = jnp.where(hit, rank + shift, -1)
            rows_x.append(jnp.sum(jnp.where((lane_p >= base) & (lane_p < base + chunks), pool_id * pool_chunks + off + lane_p - base, 0).astype(F32),
                                  axis=0, keepdims=True))
            tab_y = jnp.where((lane_p >= off) & (lane_p < off + chunks), e * cap_chunks + base + lane_p - off, tab_y)
            tab_s = jnp.where(lane_s == e, lo, tab_s)
            tab_s = jnp.where(lane_s == local + e, lo + count, tab_s)
            tab_s = jnp.where(lane_s == 2 * local + e, shift - lo, tab_s)
            off = off + chunks
            lo = lo + count
        tab_ref[layer, 0:group, :] = tab_s
        tab_ref[layer, group:group + pools, :] = tab_y
        rows_x.append(jnp.zeros((8 - local, tok), F32))
        tab_ref[layer, group + pools:group + pools + 8, :] = to_int(jnp.concatenate(rows_x, axis=0))


def tables(ids_all, layers, top, local, pool_chunks, cap_chunks):
    group, _, tok = ids_all.shape
    vm = pl.BlockSpec(memory_space=pltpu.VMEM)
    return pl.pallas_call(
        functools.partial(tables_kernel, (layers, group, top, tok, local, pool_chunks, cap_chunks)),
        out_shape=(jax.ShapeDtypeStruct((layers * local, group, tok), jnp.int32),
                   jax.ShapeDtypeStruct((layers, group + group // 2 + 8, tok), jnp.int32)),
        in_specs=[vm], out_specs=(vm, vm), name='tables',
    )(ids_all)


OFFS = (0, 1, -1, 2)
IDX = {0: 0, 1: 1, -1: 2, 2: 3}
BACK = {1: -1, -1: 1, 2: 2}


def moe_kernel(layer, dims, u_ref, a_ref, gs_ref, key_ref, tab_ref, wg_hbm, wu_hbm, wd_hbm, x_ref,
               ubuf, xg, xs, act, yq, pick, rbuf, vbuf, gmat, part, final, gsbuf, wg, wu, wd,
               ag_send, ag_recv, dd_send, dd_recv, gs_send, gs_recv, p1_send, p1_recv, p2_send, p2_recv, wsem):
    ny, nx, tok, width, local, top, pool_chunks, cap_chunks = dims
    pools = ny * nx
    group = 2 * pools
    pool_rows = pool_chunks * CHUNK
    half = tok // 2
    quarter = width // 4
    y = lax.axis_index('pool')
    ep = lax.axis_index('ep')
    x = ep // 2
    core = lax.rem(ep, 2)
    other = 1 - core

    def mod(v, n):
        return lax.rem(v + n, n)

    def at(dx, dy):
        return mod(x + dx, nx), mod(y + dy, ny)

    def dev(dx, dy, c):
        px, py = at(dx, dy)
        return {'pool': py, 'ep': px * 2 + c}

    def number(dx, dy, c):
        px, py = at(dx, dy)
        return py * (2 * nx) + px * 2 + c

    def axes(h, first, second):
        return (first, second) if h == 0 else (second, first)

    w_copies = [[pltpu.make_async_copy(src.at[layer, e], dst.at[e], wsem.at[i, e])
                 for i, (src, dst) in enumerate(((wg_hbm, wg), (wu_hbm, wu), (wd_hbm, wd)))] for e in range(local)]

    barrier = pltpu.get_barrier_semaphore()
    partners = [(0, 0, other)]
    for d in OFFS[1:]:
        for c in (0, 1):
            partners += [(d, 0, c), (0, d, c)]
    for dx, dy, c in partners:
        pl.semaphore_signal(barrier, inc=1, device_id=dev(dx, dy, c), device_id_type=MESH)
    pl.semaphore_wait(barrier, len(partners))

    def piece(h, r, q, p=None):
        if q == 0:
            step = 1 if (r == -1 or (r == 2 and p == 0)) else -1
            own = (0, 0) if r in (1, -1) else (-step, 0)
            to = (step, 0)
        else:
            step = 1 if (q == -1 or (q == 2 and p == 0)) else -1
            own = (r, 0) if q in (1, -1) else (r, -step)
            to = (0, step)
        rows = pl.ds(h * half, half) if p is None else pl.ds(h * half + p * (half // 2), half // 2)
        owner = number(*axes(h, *own), core)
        src = u_ref.at[rows] if own == (0, 0) else ubuf.at[owner, rows]
        sem = ((h * 4 + IDX[r]) * 4 + IDX[q]) * 2 + (p or 0)
        return pltpu.make_async_remote_copy(
            src_ref=src, dst_ref=ubuf.at[owner, rows], send_sem=ag_send.at[sem], recv_sem=ag_recv.at[sem],
            device_id=dev(*axes(h, *to), core), device_id_type=MESH)

    def across(h, r, q):
        rows = pl.ds(h * half, half)
        owner = number(*axes(h, r, q), core)
        src = u_ref.at[rows] if (r, q) == (0, 0) else ubuf.at[owner, rows]
        sem = (h * 4 + IDX[r]) * 4 + IDX[q]
        return pltpu.make_async_remote_copy(
            src_ref=src, dst_ref=ubuf.at[owner, rows], send_sem=dd_send.at[sem], recv_sem=dd_recv.at[sem],
            device_id=dev(0, 0, other), device_id_type=MESH)

    def gate_copy(h, q):
        back = IDX[BACK[q]]
        sem = h * 4 + back
        return pltpu.make_async_remote_copy(
            src_ref=gs_ref, dst_ref=gsbuf.at[h, back], send_sem=gs_send.at[sem], recv_sem=gs_recv.at[sem],
            device_id=dev(*axes(h, 0, q), core), device_id_type=MESH)

    started = []

    def go(copy):
        copy.start()
        started.append(copy)

    have = set()
    done = set()
    prow = lax.broadcasted_iota(jnp.int32, (pool_rows, tok), 0)

    def gather(dx, dy):
        px, py = at(dx, dy)
        chip = py * nx + px
        across(0, dx, dy).wait_recv()
        across(1, dy, dx).wait_recv()
        halves = []
        for par in range(2):
            hit = None
            for e in range(local):
                this = prow == key_ref[layer * local + e, pl.ds(2 * chip + par, 1), :]
                hit = this if hit is None else hit | this
            halves.append(jnp.where(hit, 1.0, 0.0).astype(BF16))
        onehot = jnp.concatenate(halves, axis=1)
        rows = ubuf[pl.ds(2 * chip, 2)].reshape(2 * tok, width)
        xg[pl.ds(chip * pool_chunks, pool_chunks)] = dot(onehot, rows).astype(BF16).reshape(pool_chunks, CHUNK, width)

    def ready(limit):
        for dy in OFFS:
            for dx in OFFS:
                if limit and (dx, dy) not in done and (0, dx, dy) in have and (1, dy, dx) in have:
                    done.add((dx, dy))
                    gather(dx, dy)
                    limit -= 1

    for h in (0, 1):
        go(piece(h, -1, 0))
        go(piece(h, 1, 0))
    for h in (0, 1):
        go(across(h, 0, 0))
        go(piece(h, 0, -1))
        go(piece(h, 0, 1))
    for h in (0, 1):
        for q in OFFS[1:]:
            go(gate_copy(h, q))
        have.add((h, 0, 0))
    for e in range(local):
        for cp in w_copies[e]:
            cp.start()
    ubuf[number(0, 0, core)] = u_ref[...]

    for r, p in ((-1, 0), (1, 1)):
        for h in (0, 1):
            piece(h, r, 0).wait_recv()
            go(piece(h, 2, 0, p))
            go(piece(h, r, -1))
            go(piece(h, r, 1))
            go(across(h, r, 0))
            have.add((h, r, 0))
        ready(1)
    for h in (0, 1):
        piece(h, 2, 0, 0).wait_recv()
        piece(h, 2, 0, 1).wait_recv()
        go(piece(h, 2, -1))
        go(piece(h, 2, 1))
        go(across(h, 2, 0))
        have.add((h, 2, 0))
    for r in OFFS:
        for q, p in ((-1, 0), (1, 1)):
            for h in (0, 1):
                piece(h, r, q).wait_recv()
                go(piece(h, r, 2, p))
                go(across(h, r, q))
                have.add((h, r, q))
            ready(1)
    for r in OFFS:
        for h in (0, 1):
            piece(h, r, 2, 0).wait_recv()
            piece(h, r, 2, 1).wait_recv()
            go(across(h, r, 2))
            have.add((h, r, 2))
        ready(2)
    ready(pools)

    tab_y0 = group
    tab_x0 = group + pools
    for e in range(local):
        def move(i, carry, e=e):
            xs[e * cap_chunks + i] = xg[tab_ref[layer, tab_x0 + e, i]]
            return carry
        lax.fori_loop(0, cap_chunks, move, 0, unroll=8)
    per = TILE // CHUNK
    for e in range(local):
        for cp in w_copies[e]:
            cp.wait()

        def tile(i, carry, e=e):
            rows = pl.ds(e * cap_chunks + i * per, per)
            rows_in = xs[rows].reshape(TILE, width)
            first = dot(rows_in, wg[e])
            second = dot(rows_in, wu[e])
            act[pl.ds(e * (cap_chunks // per) + i, 1)] = (first * (1.0 / (1.0 + jnp.exp(-first))) * second).astype(BF16)[None]
            return carry

        lax.fori_loop(0, cap_chunks // per, tile, 0)

    jrow = lax.broadcasted_iota(jnp.int32, (WINDOW, pool_rows), 0)
    diff = lax.broadcasted_iota(jnp.int32, (WINDOW, pool_rows), 1) - jrow

    def choose(chip, carry):
        halves = []
        for par in range(2):
            hit = None
            for e in range(local):
                lo = tab_ref[layer, 2 * chip + par, e]
                hi = tab_ref[layer, 2 * chip + par, local + e]
                delta = tab_ref[layer, 2 * chip + par, 2 * local + e]
                this = (diff == delta) & (jrow >= lo) & (jrow < hi)
                hit = this if hit is None else hit | this
            halves.append(jnp.where(hit, 1.0, 0.0).astype(BF16))
        pick[chip] = jnp.concatenate(halves, axis=0)
        return carry

    lax.fori_loop(0, pools, choose, 0)

    def first_copy(h, w, r, flip):
        c = other if flip else core
        mine = (x, y)[h]
        there = at(r, r)[h]
        sem = ((h * 2 + w) * 4 + IDX[r]) * 2 + flip
        return pltpu.make_async_remote_copy(
            src_ref=rbuf.at[h * 2 + w, there, c], dst_ref=vbuf.at[h * 2 + w, mine, core],
            send_sem=p1_send.at[sem], recv_sem=p1_recv.at[sem], device_id=dev(*axes(h, r, 0), c), device_id_type=MESH)

    def second_copy(h, w, q):
        sem = (h * 2 + w) * 4 + IDX[q]
        return pltpu.make_async_remote_copy(
            src_ref=part.at[h * 2 + w, IDX[q]], dst_ref=final.at[h * 2 + w, IDX[q]],
            send_sem=p2_send.at[sem], recv_sem=p2_recv.at[sem], device_id=dev(*axes(h, 0, q), core), device_id_type=MESH)

    firsts = [(2, 0), (2, 1), (1, 0), (-1, 0), (1, 1), (-1, 1), (0, 1)]
    order = [(0, 0), (1, 0), (0, 1), (1, 1)]
    for h, w in order:
        n = h * 2 + w
        cols = slice(n * quarter, (n + 1) * quarter)
        for e in range(local):
            def down(i, carry, e=e):
                out = dot(act[e * (cap_chunks // per) + i], wd[e, :, cols])
                yq[pl.ds(e * cap_chunks + i * per, per)] = out.astype(BF16).reshape(per, CHUNK, quarter)
                return carry
            lax.fori_loop(0, cap_chunks // per, down, 0)

        def window(chip, carry):
            rows = jnp.concatenate([yq[tab_ref[layer, tab_y0 + chip, i]] for i in range(pool_chunks)], axis=0)
            out = dot(pick[chip], rows).astype(BF16)
            cy = chip // nx
            cx = chip % nx
            one, two = (cx, cy) if h == 0 else (cy, cx)
            for par in range(2):
                rbuf[n, one, par, two] = out[par * WINDOW:(par + 1) * WINDOW]
            return carry

        lax.fori_loop(0, pools, window, 0)
        mine = (x, y)[h]
        vbuf[n, mine, core] = rbuf[n, mine, core]
        for r, flip in firsts:
            go(first_copy(h, w, r, flip))

    slots = vbuf.shape[1] * vbuf.shape[2] * WINDOW
    srow = lax.broadcasted_iota(jnp.int32, (slots, tok), 0)
    for h in (0, 1):
        for q in OFFS:
            if q:
                gate_copy(h, BACK[q]).wait_recv()
                gs = gsbuf[h, IDX[q]]
            else:
                gs = gs_ref[...]
            slot = gs[top:2 * top].astype(jnp.int32)
            if h == 0:
                rel = slot - y * slots
            else:
                source = lax.shift_right_logical(slot, 6)
                sx = lax.shift_right_logical(source, 1) & (nx - 1)
                sy = source // (2 * nx)
                rel = jnp.where(sx == x, (sy * 2 + (source & 1)) * WINDOW + (slot & (WINDOW - 1)), -1)
            g = jnp.zeros((slots, tok), F32)
            for k in range(top):
                g = jnp.where(srow == rel[k:k + 1], gs[k:k + 1], g)
            for i, v in enumerate(split3(jnp.transpose(g))):
                gmat[h * 4 + IDX[q], i * tok:(i + 1) * tok, :] = v

    for h, w in order:
        n = h * 2 + w
        for r, flip in firsts:
            first_copy(h, w, r, flip).wait_recv()
        for q in (2, 1, -1, 0):
            two = at(q, q)[1 - h]
            parts = dot(gmat[h * 4 + IDX[q]], vbuf[n, :, :, two].reshape(slots, quarter))
            part[n, IDX[q]] = parts[0:tok] + parts[tok:2 * tok] + parts[2 * tok:3 * tok]
            if q:
                go(second_copy(h, w, q))
    for h, w in order:
        n = h * 2 + w
        cols = slice(n * quarter, (n + 1) * quarter)
        for q in OFFS[1:]:
            second_copy(h, w, q).wait_recv()
        total = (part[n, 0] + final[n, 1]) + (final[n, 2] + final[n, 3])
        x_ref[:, cols] = (a_ref[:, cols].astype(F32) + total).astype(BF16)
    for copy in started:
        copy.wait_send()


def moe(layer, mesh_dims, a, u, gs, keys, tab, w_gate, w_up, w_down, pool_chunks, cap_chunks):
    ny, nx = mesh_dims
    tok, width = u.shape
    top = gs.shape[0] // 2
    local, ff = w_gate.shape[1], w_gate.shape[3]
    pools = ny * nx
    group = 2 * pools
    quarter = width // 4
    per = TILE // CHUNK
    vm = pl.BlockSpec(memory_space=pltpu.VMEM)
    hb = pl.BlockSpec(memory_space=pl.ANY)
    sm = pl.BlockSpec(memory_space=pltpu.SMEM)
    sem = pltpu.SemaphoreType.DMA
    return pl.pallas_call(
        functools.partial(moe_kernel, layer, (ny, nx, tok, width, local, top, pool_chunks, cap_chunks)),
        out_shape=jax.ShapeDtypeStruct((tok, width), BF16),
        in_specs=[vm, vm, vm, vm, sm, hb, hb, hb],
        out_specs=vm,
        scratch_shapes=[
            pltpu.VMEM((group, tok, width), BF16),
            pltpu.VMEM((pools * pool_chunks, CHUNK, width), BF16),
            pltpu.VMEM((local * cap_chunks, CHUNK, width), BF16),
            pltpu.VMEM((local * cap_chunks // per, TILE, ff), BF16),
            pltpu.VMEM((local * cap_chunks, CHUNK, quarter), BF16),
            pltpu.VMEM((pools, 2 * WINDOW, pool_chunks * CHUNK), BF16),
            pltpu.VMEM((4, nx, 2, ny, WINDOW, quarter), BF16),
            pltpu.VMEM((4, nx, 2, ny, WINDOW, quarter), BF16),
            pltpu.VMEM((8, 3 * tok, 2 * nx * WINDOW), BF16),
            pltpu.VMEM((4, 4, tok, quarter), F32),
            pltpu.VMEM((4, 4, tok, quarter), F32),
            pltpu.VMEM((2, 4) + gs.shape, F32),
            pltpu.VMEM((local, width, ff), BF16), pltpu.VMEM((local, width, ff), BF16), pltpu.VMEM((local, ff, width), BF16),
            sem((64,)), sem((64,)), sem((32,)), sem((32,)), sem((8,)), sem((8,)), sem((32,)), sem((32,)), sem((16,)), sem((16,)), sem((3, local)),
        ],
        compiler_params=pltpu.CompilerParams(vmem_limit_bytes=VMEM_LIMIT, collective_id=layer, has_side_effects=True),
        cost_estimate=pl.CostEstimate(flops=6 * 10 ** 9, bytes_accessed=20 * 10 ** 6, transcendentals=0),
        name='moe',
    )(u, a, gs, keys, tab, w_gate, w_up, w_down)


def solution(mesh):
    ny, nx = mesh.shape['pool'], mesh.shape['ep'] // 2

    def device_step(hidden, k_cache, v_cache, lengths, w_query, w_key, w_value, w_out, w_router, expert_ids, w_gate, w_up, w_down):
        tok, width = hidden.shape
        layers, _, top = expert_ids.shape
        local = w_gate.shape[1]
        group = 2 * nx * ny
        pools = nx * ny
        k_cache = k_cache.reshape(layers, tok, k_cache.shape[2], k_cache.shape[4])
        v_cache = v_cache.reshape(k_cache.shape)
        mine = jnp.swapaxes(expert_ids, 1, 2).reshape(layers * top, tok)
        pool_chunks = (2 * (WINDOW - 1) + local * (CHUNK - 1)) // CHUNK
        most = 2 * group * tok * top // (group * local)
        cap_chunks = pl.cdiv((most + pools * (CHUNK - 1)) // CHUNK, TILE // CHUNK) * (TILE // CHUNK)
        for layer in range(layers):
            out = attention(layer, None if layer else (ny, 2 * nx), hidden, k_cache, v_cache, lengths, w_query, w_key, w_value, w_out, w_router,
                            expert_ids[layer], mine, local)
            if layer == 0:
                keys, tab = tables(out[3], layers, top, local, pool_chunks, cap_chunks)
            a, u, gs = out[:3]
            hidden = moe(layer, (ny, nx), a, u, gs, keys, tab, w_gate, w_up, w_down, pool_chunks, cap_chunks)
        return hidden

    cache_spec = P(None, BATCH_AXES, None, None, None)
    expert_spec = P(None, GROUP_AXES, None, None)
    in_specs = (P(BATCH_AXES, None), cache_spec, cache_spec, P(BATCH_AXES), P(), P(), P(), P(), P(), P(None, BATCH_AXES, None), expert_spec, expert_spec, expert_spec)
    return jax.shard_map(device_step, mesh=mesh, in_specs=in_specs, out_specs=P(BATCH_AXES, None), check_vma=False)
```

time: 396 us -> 242 us (0.61)
  waiting for transfers between devices: 119 us -> 0 us
  blocking collectives: 94.1 us -> 0 us
  Pallas kernels: 155 us -> 235 us
  between operations: 13.5 us -> 0.22 us
  starting transfers between devices: 9.08 us -> 0 us
    pallas_call x6 -> x4, Pallas kernels: 153 us -> 232 us  [the longest x2 193 us: moe(): pl.pallas_call(functools.partial(moe_kernel, layer, (ny, nx, tok, width,...]
    all_gather x2 -> x0, waiting for transfers between devices: 67.3 us -> none  [device_step(): u_all = lax.all_gather(u, GROUP_AXES, axis=0)]
    all_to_all x1 -> x0, blocking collectives: 61.6 us -> none  [device_step(): back = lax.all_to_all(rows, GROUP_AXES, 0, 0, tiled=True)]
    all_to_all x1 -> x0, waiting for transfers between devices: 51.4 us -> none  [device_step(): back = lax.all_to_all(rows, GROUP_AXES, 0, 0, tiled=True)]
    all_gather x1 -> x0, blocking collectives: 32.5 us -> none  [device_step(): lax.all_gather(jnp.swapaxes(expert_ids, 1, 2).reshape(layers * top, tok),...]
    all_to_all x1 -> x0, starting transfers between devices: 9.02 us -> none  [device_step(): back = lax.all_to_all(rows, GROUP_AXES, 0, 0, tiled=True)]
  transfers between devices with their start and end apart: 3 -> 0, of which waited for: 3 -> 0; matrix products, arithmetic and copies ran while one was open for 0% -> 0% of each run, Pallas kernels for 1% -> 0%
where the time goes in v2:
time: 242 us; the launch traced here: 239 us
  Pallas kernels  235 us (97%)
  local copies, waits for them, and re-layouts  3.84 us (2%)
    pallas_call x2, Pallas kernels, moe(): pl.pallas_call(functools.partial(moe_kernel, layer, (ny, nx, tok, width,...  193 us
    pallas_call x2, Pallas kernels, attention(): pl.pallas_call(functools.partial(attention_kernel, layer, dims, share), o...  38.5 us

profile of v2, /device:TPU:97, one launch (start us, length us, event | category | flops | bytes accessed | tf_op | source)
XLA Modules:
  0.0 239.3 jit_solution(11890051112557741294)
XLA Ops:
  0.0 0.7 fusion
  0.7 0.7 copy.17
  1.4 0.7 copy.16
  2.2 22.2 %attention.2 = (bf16[128,1024]{1,0:T(8,128)(2,1)}, bf16[128,1024]{1,0:T(8,128)(2,1)}, f32[16,128]{1,0:T(8,128)}, s32[32,16,128]{2,1,0:T(8,128)}) custom-call(bf16[128,1024]{1,0:T(8,128)(2,1)} %hidden_ref.1, bf16[2,128,128,128]{3,2,1,0:T(8,128)(2,1)} %bitcast.7, bf16[2,128,128,128]{3,2,1,0:T(8,128)(2,1)} %bitcast.9, s32[128]{0:T(128)} %len_ref.3, ...), custom_call_target="tpu_custom_call" | custom-call | flops 4000000000 | bytes 20000000 | tf_op jit(solution)/shard_map/attention/pallas_call | solution.py:208
  24.4 3.4 %tables.1 = (s32[8,32,128]{2,1,0:T(8,128)}, s32[2,56,128]{2,1,0:T(8,128)}) custom-call(s32[32,16,128]{2,1,0:T(8,128)} %get-tuple-element.17.ids_ref), custom_call_target="tpu_custom_call" | custom-call | tf_op jit(solution)/shard_map/tables/pallas_call | solution.py:290
  27.8 96.9 %moe.2.hidden_ref = bf16[128,1024]{1,0:T(8,128)(2,1)} custom-call(bf16[128,1024]{1,0:T(8,128)(2,1)} %get-tuple-element.14.u_ref, bf16[128,1024]{1,0:T(8,128)(2,1)} %get-tuple-element.15.a_ref, f32[16,128]{1,0:T(8,128)} %get-tuple-element.16.gs_ref, s32[8,32,128]{2,1,0:T(8,128)} %get-tuple-element.18.key_ref, s32[2,56,128]{2,1,0:T(8,128)} %get-tuple-element.19.tab_ref, ...), custom_call_target="tpu_custom_call" | custom-call | flops 6000000000 | bytes 20000000 | tf_op jit(solution)/shard_map/moe/pallas_call | solution.py:604
  124.7 16.2 %attention.3 = (bf16[128,1024]{1,0:T(8,128)(2,1)}, bf16[128,1024]{1,0:T(8,128)(2,1)}, f32[16,128]{1,0:T(8,128)}) custom-call(bf16[128,1024]{1,0:T(8,128)(2,1)} %moe.2.hidden_ref, bf16[2,128,128,128]{3,2,1,0:T(8,128)(2,1)} %bitcast.8, bf16[2,128,128,128]{3,2,1,0:T(8,128)(2,1)} %bitcast.10, s32[128]{0:T(128)} %len_ref.3, bf16[2,1024,2048]{2,1,0:T(8,128)(2,1)} %wq_hbm.3, ...), custom_call_target="tpu_custom_call" | custom-call | flops 4000000000 | bytes 20000000 | tf_op jit(solution)/shard_map/attention/pallas_call | solution.py:208
  141.0 96.5 %moe.3 = bf16[128,1024]{1,0:T(8,128)(2,1)} custom-call(bf16[128,1024]{1,0:T(8,128)(2,1)} %get-tuple-element.20.u_ref, bf16[128,1024]{1,0:T(8,128)(2,1)} %get-tuple-element.21.a_ref, f32[16,128]{1,0:T(8,128)} %get-tuple-element.22.gs_ref, s32[8,32,128]{2,1,0:T(8,128)} %get-tuple-element.18.key_ref, s32[2,56,128]{2,1,0:T(8,128)} %get-tuple-element.19.tab_ref, ...), custom_call_target="tpu_custom_call" | custom-call | flops 6000000000 | bytes 20000000 | tf_op jit(solution)/shard_map/moe/pallas_call | solution.py:604
  237.4 1.7 copy.19

commit v3 on v0

v3 whole, which is shorter than its diff:
```python
import functools

import jax
import jax.numpy as jnp
from jax import lax
from jax.experimental import pallas as pl
from jax.experimental.pallas import tpu as pltpu
from jax.sharding import PartitionSpec as P

EPS = 1e-6
GROUP_AXES = ('pool', 'ep')
BATCH_AXES = ('dp', 'pool', 'ep')
F32 = jnp.float32
BF16 = jnp.bfloat16
I32 = jnp.int32
CHUNK = 16
WINDOW = 64
TILE = 256
LANES = 128
BLOCK = 16
WAVES = 2
MESH = pl.DeviceIdType.MESH
OFFS = (0, -1, 1, 2)
IDX = {0: 0, 1: 1, -1: 2, 2: 3}
BACK = {1: -1, -1: 1, 2: 2}


def rms_norm(wide):
    return (wide * lax.rsqrt(jnp.mean(wide * wide, axis=-1, keepdims=True) + EPS)).astype(BF16)


def dot(a, b):
    return jnp.dot(a, b, preferred_element_type=F32)


def dot_t(a, b):
    return lax.dot_general(a, b, (((1,), (1,)), ((), ())), preferred_element_type=F32)


def split3(w):
    hi = w.astype(BF16)
    rest = w - hi.astype(F32)
    mid = rest.astype(BF16)
    low = (rest - mid.astype(F32)).astype(BF16)
    return hi, mid, low


def iota(shape, axis):
    return lax.broadcasted_iota(I32, shape, axis)


def onehot(cond):
    return jnp.where(cond, 1.0, 0.0).astype(BF16)


def step_kernel(dims, hidden_ref, kc_hbm, vc_hbm, len_ref, wq_hbm, wk_hbm, wv_hbm, wo_hbm, wr_hbm, cols_ref, mine_ref, wg_hbm, wu_hbm, wd_hbm,
                x_ref,
                xcur, abuf, ubuf0, gs, q3, o3, sbuf, nbuf, kn3, vn3, wq, wk, wv, wo, wr,
                idsbuf, keys, tabv, tab, ubuf, xg, xt, act, yq, pick, rbuf, vbuf, gmat, part, final, gsbuf, wg, wu, wd,
                ksem, vsem, asem, wsem, tsem, id_send, id_recv, ag_send, ag_recv, dd_send, dd_recv, gs_send, gs_recv,
                p1_send, p1_recv, p2_send, p2_recv):
    ny, nx, layers, tok, width, heads, hd, seq, experts, local, top, pool_chunks, cap_chunks = dims
    pools = ny * nx
    group = 2 * pools
    pool_rows = pool_chunks * CHUNK
    span = tok // WAVES
    half = span // 2
    quarter = width // 4
    lane_tiles = quarter // LANES
    per = TILE // CHUNK
    per_expert = cap_chunks // per
    slots = 2 * nx * WINDOW
    y = lax.axis_index('pool')
    ep = lax.axis_index('ep')
    x = ep // 2
    core = lax.rem(ep, 2)
    other = 1 - core
    me = y * (2 * nx) + ep

    def at(dx, dy):
        return lax.rem(x + dx + nx, nx), lax.rem(y + dy + ny, ny)

    def dev(dx, dy, c):
        px, py = at(dx, dy)
        return {'pool': py, 'ep': px * 2 + c}

    def number(dx, dy, c):
        px, py = at(dx, dy)
        return py * (2 * nx) + px * 2 + c

    def axes(h, first, second):
        return (first, second) if h == 0 else (second, first)

    def peer(d):
        to = lax.rem(me + d, group)
        return {'pool': to // (2 * nx), 'ep': lax.rem(to, 2 * nx)}

    def remote(src, dst, send, recv, device):
        return pltpu.make_async_remote_copy(src_ref=src, dst_ref=dst, send_sem=send, recv_sem=recv, device_id=device, device_id_type=MESH)

    def att_copies(layer):
        return [pltpu.make_async_copy(src.at[layer], dst, asem.at[i])
                for i, (src, dst) in enumerate(((wq_hbm, wq), (wk_hbm, wk), (wv_hbm, wv), (wo_hbm, wo), (wr_hbm, wr)))]

    def expert_copies(layer):
        return [pltpu.make_async_copy(src.at[layer, e], dst.at[e], wsem.at[i, e])
                for i, (src, dst) in enumerate(((wg_hbm, wg), (wu_hbm, wu), (wd_hbm, wd))) for e in range(local)]

    def kv_copies(layer, b):
        rows = pl.ds(b * (BLOCK * seq), BLOCK * seq)
        return (pltpu.make_async_copy(kc_hbm.at[layer, rows], rbuf.at[rows], ksem.at[b]),
                pltpu.make_async_copy(vc_hbm.at[layer, rows], vbuf.at[rows], vsem.at[b]))

    def id_copy(d):
        return remote(mine_ref, idsbuf.at[me], id_send.at[d], id_recv.at[d], peer(d))

    def piece(w, h, r, q, p=None):
        if q == 0:
            step = 1 if (r == -1 or (r == 2 and p == 0)) else -1
            own = (0, 0) if r in (1, -1) else (-step, 0)
            to = (step, 0)
        else:
            step = 1 if (q == -1 or (q == 2 and p == 0)) else -1
            own = (r, 0) if q in (1, -1) else (r, -step)
            to = (0, step)
        first = w * span + h * half
        rows = pl.ds(first, half) if p is None else pl.ds(first + p * (half // 2), half // 2)
        owner = number(*axes(h, *own), core)
        src = ubuf0.at[rows] if own == (0, 0) else ubuf.at[owner, rows]
        sem = (((w * 2 + h) * 4 + IDX[r]) * 4 + IDX[q]) * 2 + (p or 0)
        return remote(src, ubuf.at[owner, rows], ag_send.at[sem], ag_recv.at[sem], dev(*axes(h, *to), core))

    def across(w, h, r, q):
        rows = pl.ds(w * span + h * half, half)
        owner = number(*axes(h, r, q), core)
        src = ubuf0.at[rows] if (r, q) == (0, 0) else ubuf.at[owner, rows]
        sem = ((w * 2 + h) * 4 + IDX[r]) * 4 + IDX[q]
        return remote(src, ubuf.at[owner, rows], dd_send.at[sem], dd_recv.at[sem], dev(0, 0, other))

    def gate_copy(h, q):
        back = IDX[BACK[q]]
        sem = h * 4 + back
        return remote(gs, gsbuf.at[h, back], gs_send.at[sem], gs_recv.at[sem], dev(*axes(h, 0, q), core))

    def window_row(n, one, c, two=0):
        return ((n * nx + one) * 2 + c) * (ny * lane_tiles * WINDOW) + two * (lane_tiles * WINDOW)

    def first_copy(h, w, r, flip):
        n = h * 2 + w
        c = other if flip else core
        size = ny * lane_tiles * WINDOW
        src = pl.ds(pl.multiple_of(window_row(n, at(r, r)[h], c), size), size)
        dst = pl.ds(pl.multiple_of(window_row(n, (x, y)[h], core), size), size)
        sem = (n * 4 + IDX[r]) * 2 + flip
        return remote(rbuf.at[src], vbuf.at[dst], p1_send.at[sem], p1_recv.at[sem], dev(*axes(h, r, 0), c))

    def second_copy(h, w, q):
        n = h * 2 + w
        sem = n * 4 + IDX[q]
        return remote(part.at[n, IDX[q]], final.at[n, IDX[q]], p2_send.at[sem], p2_recv.at[sem], dev(*axes(h, 0, q), core))

    for cp in att_copies(0):
        cp.start()
    barrier = pltpu.get_barrier_semaphore()
    for d in range(1, group):
        pl.semaphore_signal(barrier, inc=1, device_id=peer(d), device_id_type=MESH)
    pl.semaphore_wait(barrier, group - 1)
    for d in range(1, group):
        id_copy(d).start()
    idsbuf[me] = mine_ref[...]
    xcur[...] = hidden_ref[...]
    scale = hd ** -0.5
    lane = iota((heads, seq), 1)

    def layer_body(layer, carry):
        for b in range(tok // BLOCK):
            for cp in kv_copies(layer, b):
                cp.start()
        for cp in expert_copies(layer):
            cp.start()
        normed = rms_norm(xcur[...].astype(F32))
        for cp in att_copies(layer)[:3]:
            cp.wait()
        kn3[...] = dot(normed, wk[...]).astype(BF16).astype(F32)
        vn3[...] = dot(normed, wv[...]).astype(BF16).astype(F32)
        for h in range(heads):
            if h % 2 == 0:
                pair = dot(normed, wq[:, h * hd:(h + 2) * hd])
            q3[:, h, :] = pair[:, (h % 2) * hd:(h % 2 + 1) * hd].astype(BF16).astype(F32)

        def block(b, c2):
            kcp, vcp = kv_copies(layer, b)
            kcp.wait()
            for j in range(BLOCK):
                t = b * BLOCK + j
                q = q3[t]
                s = dot_t(q.astype(BF16), rbuf[pl.ds(t * seq, seq), :]) * scale
                sbuf[j * heads:(j + 1) * heads, :] = jnp.where(lane < len_ref[t], s, -jnp.inf)
                nbuf[j * heads:(j + 1) * heads, :] = q * kn3[pl.ds(t, 1), :]
            s = sbuf[...]
            sn = jnp.sum(nbuf[...], axis=1, keepdims=True) * scale
            peak = jnp.maximum(jnp.max(s, axis=1, keepdims=True), sn)
            p = jnp.exp(s - peak)
            pn = jnp.exp(sn - peak)
            inv = 1.0 / (jnp.sum(p, axis=1, keepdims=True) + pn)
            pb = (p * inv).astype(BF16)
            pnb = (pn * inv).astype(BF16).astype(F32)
            vcp.wait()
            for j in range(BLOCK):
                t = b * BLOCK + j
                rows = slice(j * heads, (j + 1) * heads)
                o = dot(pb[rows], vbuf[pl.ds(t * seq, seq), :]) + pnb[rows] * vn3[pl.ds(t, 1), :]
                o3[t] = o.astype(BF16).astype(F32)
            return c2

        def project(w):
            rows = slice(w * span, (w + 1) * span)
            mixed = jnp.concatenate([o3[rows, h, :].astype(BF16) for h in range(heads)], axis=1)
            a = (xcur[rows].astype(F32) + dot(mixed, wo[...])).astype(BF16)
            abuf[rows] = a
            ubuf0[rows] = rms_norm(a.astype(F32))

        started = []

        def go(fn, *args):
            fn(*args).start()
            started.append((fn, args))

        have = set()
        done = set()
        prow = iota((pool_rows, tok), 0)

        def gather(dx, dy):
            px, py = at(dx, dy)
            chip = py * nx + px
            for w in range(WAVES):
                across(w, 0, dx, dy).wait_recv()
                across(w, 1, dy, dx).wait_recv()
            halves = []
            for par in range(2):
                hit = None
                for e in range(local):
                    this = prow == keys[e, pl.ds(2 * chip + par, 1), :]
                    hit = this if hit is None else hit | this
                halves.append(onehot(hit))
            rows = ubuf[pl.ds(2 * chip, 2)].reshape(2 * tok, width)
            xg[pl.ds(chip * pool_chunks, pool_chunks)] = dot(jnp.concatenate(halves, axis=1), rows).astype(BF16).reshape(pool_chunks, CHUNK, width)

        def ready(limit):
            for dy in OFFS:
                for dx in OFFS:
                    if limit and (dx, dy) not in done and all((w, 0, dx, dy) in have and (w, 1, dy, dx) in have for w in range(WAVES)):
                        done.add((dx, dy))
                        gather(dx, dy)
                        limit -= 1

        def s0(w):
            for h in (0, 1):
                go(piece, w, h, -1, 0)
                go(piece, w, h, 1, 0)
            for h in (0, 1):
                go(piece, w, h, 0, -1)
                go(piece, w, h, 0, 1)
                go(across, w, h, 0, 0)
                have.add((w, h, 0, 0))

        def s2(w):
            for r, p in ((-1, 0), (1, 1)):
                for h in (0, 1):
                    piece(w, h, r, 0).wait_recv()
                    go(piece, w, h, 2, 0, p)
                    go(piece, w, h, r, -1)
                    go(piece, w, h, r, 1)
                    go(across, w, h, r, 0)
                    have.add((w, h, r, 0))

        def s3(w):
            for h in (0, 1):
                piece(w, h, 2, 0, 0).wait_recv()
                piece(w, h, 2, 0, 1).wait_recv()
                go(piece, w, h, 2, -1)
                go(piece, w, h, 2, 1)
                go(across, w, h, 2, 0)
                have.add((w, h, 2, 0))

        def s4(w, r):
            for q, p in ((-1, 0), (1, 1)):
                for h in (0, 1):
                    piece(w, h, r, q).wait_recv()
                    go(piece, w, h, r, 2, p)
                    go(across, w, h, r, q)
                    have.add((w, h, r, q))

        def s5(w, r):
            for h in (0, 1):
                piece(w, h, r, 2, 0).wait_recv()
                piece(w, h, r, 2, 1).wait_recv()
                go(across, w, h, r, 2)
                have.add((w, h, r, 2))

        blocks = span // BLOCK
        lax.fori_loop(0, blocks, block, 0)
        att_copies(layer)[3].wait()
        project(0)
        s0(0)
        lax.fori_loop(blocks, 2 * blocks - 1, block, 0)
        s2(0)
        lax.fori_loop(2 * blocks - 1, 2 * blocks, block, 0)
        s4(0, 0)
        project(1)
        s0(1)
        s3(0)

        att_copies(layer)[4].wait()
        hi, mid, low = split3(wr[...])
        u = ubuf0[...]
        logits = dot(u, hi) + dot(u, mid) + dot(u, low)

        @pl.when(layer + 1 < layers)
        def _():
            for cp in att_copies(layer + 1):
                cp.start()

        e_iota = iota((tok, experts), 1)
        before = onehot(iota((tok, tok), 1) < iota((tok, tok), 0))
        e_row = iota((experts, experts), 0)
        e_col = iota((experts, experts), 1)
        same = onehot((e_row < e_col) & (e_row // local == e_col // local))
        hits = [cols_ref[layer, :, k:k + 1] == e_iota for k in range(top)]
        chosen = hits[0]
        for k in range(1, top):
            chosen = chosen | hits[k]
        chosen = jnp.where(chosen, 1.0, 0.0)
        rank = dot(before, chosen.astype(BF16))
        count = jnp.sum(chosen, axis=0, keepdims=True)
        start = dot(jnp.broadcast_to(count, (8, experts)).astype(BF16), same)[0:1]
        slot_full = rank + start + ((e_iota // local) * WINDOW).astype(F32)
        picked = [jnp.sum(jnp.where(hit, logits, 0.0), axis=1, keepdims=True) for hit in hits]
        peak = picked[0]
        for k in range(1, top):
            peak = jnp.maximum(peak, picked[k])
        ex = [jnp.exp(v - peak) for v in picked]
        total = ex[0]
        for k in range(1, top):
            total = total + ex[k]
        columns = [v / total for v in ex] + [jnp.sum(jnp.where(hit, slot_full, 0.0), axis=1, keepdims=True) for hit in hits]
        columns.append(jnp.zeros((tok, LANES - 2 * top), F32))
        gs[...] = jnp.transpose(jnp.concatenate(columns, axis=1))[:2 * top]
        ubuf[me] = u
        for h in (0, 1):
            for q in OFFS[1:]:
                go(gate_copy, h, q)
        s4(0, -1)
        s4(0, 1)
        s2(1)

        @pl.when(layer == 0)
        def _():
            for d in range(1, group):
                id_copy(d).wait()

        before_tok = onehot(iota((tok, tok), 0) < iota((tok, tok), 1))
        before_pool = onehot(iota((pools, pools), 1) < iota((pools, pools), 0))
        pair_of = onehot(iota((pools, group), 1) // 2 == iota((pools, group), 0))
        spread = onehot(iota((group, pools), 0) // 2 == iota((group, pools), 1))
        prev = onehot((iota((group, group), 1) + 1 == iota((group, group), 0)) & (iota((group, group), 0) % 2 == 1))
        lane_p = iota((pools, tok), 1)
        pool_id = iota((pools, tok), 0)
        lane_s = iota((group, tok), 1)
        off = jnp.zeros((pools, tok), I32)
        lo = jnp.zeros((group, tok), I32)
        tab_y = jnp.zeros((pools, tok), I32)
        tab_s = jnp.zeros((group, tok), I32)
        rows_x = []
        for e in range(local):
            target = me * local + e
            hit = idsbuf[:, layer, 0, :] == target
            for k in range(1, top):
                hit = hit | (idsbuf[:, layer, k, :] == target)
            hitb = onehot(hit)
            rank = dot(hitb, before_tok).astype(I32)
            count = jnp.broadcast_to(jnp.sum(jnp.where(hit, 1.0, 0.0), axis=1, keepdims=True), (group, tok))
            countb = count.astype(BF16)
            count = count.astype(I32)
            amount = dot(pair_of, countb).astype(I32)
            chunks = lax.shift_right_logical(amount + (CHUNK - 1), 4)
            base = dot(before_pool, chunks.astype(F32).astype(BF16)).astype(I32)
            shift = dot(spread, (off * CHUNK).astype(F32).astype(BF16)).astype(I32) + dot(prev, countb).astype(I32)
            keys[e] = jnp.where(hit, rank + shift, -1)
            rows_x.append(jnp.sum(jnp.where((lane_p >= base) & (lane_p < base + chunks), pool_id * pool_chunks + off + lane_p - base, 0).astype(F32),
                                  axis=0, keepdims=True))
            tab_y = jnp.where((lane_p >= off) & (lane_p < off + chunks), e * cap_chunks + base + lane_p - off, tab_y)
            tab_s = jnp.where(lane_s == e, lo, tab_s)
            tab_s = jnp.where(lane_s == local + e, lo + count, tab_s)
            tab_s = jnp.where(lane_s == 2 * local + e, shift - lo, tab_s)
            off = off + chunks
            lo = lo + count
        tab_y0 = group
        tab_x0 = group + pools
        tabv[0:group, :] = tab_s
        tabv[group:group + pools, :] = jnp.clip(tab_y, 0, local * cap_chunks - 1)
        rows_x.append(jnp.zeros((8 - local, tok), F32))
        tabv[tab_x0:tab_x0 + 8, :] = jnp.clip(jnp.concatenate(rows_x, axis=0).astype(I32), 0, pools * pool_chunks - 1)
        tab_copy = pltpu.make_async_copy(tabv, tab, tsem)
        tab_copy.start()

        s4(0, 2)
        s3(1)
        for r in OFFS:
            s5(0, r)
        ready(1)
        s4(1, 0)
        ready(2)

        srow = iota((slots, tok), 0)

        def gates(h):
            for q in OFFS:
                if q:
                    gate_copy(h, BACK[q]).wait_recv()
                    table = gsbuf[h, IDX[q]]
                else:
                    table = gs[...]
                slot = table[top:2 * top].astype(I32)
                if h == 0:
                    rel = slot - y * slots
                else:
                    source = lax.shift_right_logical(slot, 6)
                    sx = lax.shift_right_logical(source, 1) & (nx - 1)
                    sy = source // (2 * nx)
                    rel = jnp.where(sx == x, (sy * 2 + (source & 1)) * WINDOW + (slot & (WINDOW - 1)), -1)
                g = jnp.zeros((slots, tok), F32)
                for k in range(top):
                    g = jnp.where(srow == rel[k:k + 1], table[k:k + 1], g)
                for i, v in enumerate(split3(jnp.transpose(g))):
                    gmat[h * 4 + IDX[q], i * tok:(i + 1) * tok, :] = v

        s4(1, -1)
        gates(0)
        s4(1, 1)
        ready(2)
        tab_copy.wait()

        jrow = iota((WINDOW, pool_rows), 0)
        diff = iota((WINDOW, pool_rows), 1) - jrow

        def choose(chip, c2):
            halves = []
            for par in range(2):
                hit = None
                for e in range(local):
                    low_ = tab[2 * chip + par, e]
                    high_ = tab[2 * chip + par, local + e]
                    delta = tab[2 * chip + par, 2 * local + e]
                    this = (diff == delta) & (jrow >= low_) & (jrow < high_)
                    hit = this if hit is None else hit | this
                halves.append(onehot(hit))
            pick[chip] = jnp.concatenate(halves, axis=0)
            return c2

        lax.fori_loop(0, pools, choose, 0)
        s4(1, 2)
        ready(3)
        gates(1)
        s5(1, 0)
        ready(2)
        s5(1, -1)
        s5(1, 1)
        ready(4)
        s5(1, 2)
        ready(pools)

        for cp in expert_copies(layer):
            cp.wait()

        def tile(i, c2):
            e = i // per_expert
            first_chunk = (i % per_expert) * per
            for j in range(per):
                xt[j * CHUNK:(j + 1) * CHUNK, :] = xg[tab[tab_x0 + e, first_chunk + j]]
            rows_in = xt[...]
            first = dot(rows_in, wg[e])
            second = dot(rows_in, wu[e])
            act[i] = (first * (1.0 / (1.0 + jnp.exp(-first))) * second).astype(BF16)
            return c2

        lax.fori_loop(0, local * per_expert, tile, 0)
        for fn, args in started:
            fn(*args).wait_send()
        started.clear()

        firsts = [(2, 0), (2, 1), (1, 0), (-1, 0), (1, 1), (-1, 1), (0, 1)]
        for w in (0, 1):
            def down(i, c2):
                out = dot(act[i], wd[i // per_expert, :, 2 * w * quarter:2 * (w + 1) * quarter])
                yq[pl.ds(i * per, per)] = out.astype(BF16).reshape(per, CHUNK, 2 * quarter)
                return c2

            lax.fori_loop(0, local * per_expert, down, 0)

            def window(chip, c2):
                rows = jnp.concatenate([yq[tab[tab_y0 + chip, i]] for i in range(pool_chunks)], axis=0)
                out = dot(pick[chip], rows).astype(BF16)
                cy = chip // nx
                cx = chip % nx
                for h in (0, 1):
                    one, two = axes(h, cx, cy)
                    for par in range(2):
                        for lt in range(lane_tiles):
                            row = window_row(h * 2 + w, one, par, two) + lt * WINDOW
                            rbuf[pl.ds(pl.multiple_of(row, WINDOW), WINDOW), :] = out[par * WINDOW:(par + 1) * WINDOW,
                                                                                     h * quarter + lt * LANES:h * quarter + (lt + 1) * LANES]
                return c2

            lax.fori_loop(0, pools, window, 0)
            for r, flip in firsts:
                for h in (0, 1):
                    go(first_copy, h, w, r, flip)
            for h in (0, 1):
                size = ny * lane_tiles * WINDOW
                own = pl.ds(pl.multiple_of(window_row(h * 2 + w, (x, y)[h], core), size), size)
                vbuf[own, :] = rbuf[own, :]

        for w in (0, 1):
            for h in (0, 1):
                n = h * 2 + w
                for r, flip in firsts:
                    first_copy(h, w, r, flip).wait_recv()
                for q in (2, 1, -1, 0):
                    two = at(q, q)[1 - h]
                    rows = []
                    for s in range(2 * nx):
                        row = window_row(n, s // 2, s % 2, two)
                        rows.append(jnp.concatenate([vbuf[pl.ds(pl.multiple_of(row + lt * WINDOW, WINDOW), WINDOW), :] for lt in range(lane_tiles)], axis=1))
                    parts = dot(gmat[h * 4 + IDX[q]], jnp.concatenate(rows, axis=0))
                    part[n, IDX[q]] = parts[0:tok] + parts[tok:2 * tok] + parts[2 * tok:3 * tok]
                    if q:
                        go(second_copy, h, w, q)
        for w in (0, 1):
            for h in (0, 1):
                n = h * 2 + w
                where = slice((w * 2 + h) * quarter, (w * 2 + h + 1) * quarter)
                for q in OFFS[1:]:
                    second_copy(h, w, q).wait_recv()
                total = (part[n, 0] + final[n, 1]) + (final[n, 2] + final[n, 3])
                xcur[:, where] = (abuf[:, where].astype(F32) + total).astype(BF16)
        for fn, args in started:
            fn(*args).wait_send()
        return carry

    lax.fori_loop(0, layers, layer_body, 0)
    x_ref[...] = xcur[...]


def solution(mesh):
    ny, nx = mesh.shape['pool'], mesh.shape['ep'] // 2

    def device_step(hidden, k_cache, v_cache, lengths, w_query, w_key, w_value, w_out, w_router, expert_ids, w_gate, w_up, w_down):
        tok, width = hidden.shape
        layers, _, top = expert_ids.shape
        seq, hd = k_cache.shape[2], k_cache.shape[4]
        heads = w_query.shape[2] // hd
        experts = w_router.shape[2]
        local, ff = w_gate.shape[1], w_gate.shape[3]
        pools = nx * ny
        group = 2 * pools
        k_cache = k_cache.reshape(layers, tok * seq, hd)
        v_cache = v_cache.reshape(layers, tok * seq, hd)
        mine = jnp.swapaxes(expert_ids, 1, 2)
        pool_chunks = (2 * (WINDOW - 1) + local * (CHUNK - 1)) // CHUNK
        most = 2 * group * tok * top // (group * local)
        per = TILE // CHUNK
        cap_chunks = pl.cdiv((most + pools * (CHUNK - 1)) // CHUNK, per) * per
        quarter = width // 4
        vm = pl.BlockSpec(memory_space=pltpu.VMEM)
        hb = pl.BlockSpec(memory_space=pl.ANY)
        sm = pl.BlockSpec(memory_space=pltpu.SMEM)
        dma = pltpu.SemaphoreType.DMA
        dims = (ny, nx, layers, tok, width, heads, hd, seq, experts, local, top, pool_chunks, cap_chunks)
        return pl.pallas_call(
            functools.partial(step_kernel, dims),
            out_shape=jax.ShapeDtypeStruct((tok, width), BF16),
            in_specs=[vm, hb, hb, sm, hb, hb, hb, hb, hb, vm, vm, hb, hb, hb],
            out_specs=vm,
            scratch_shapes=[
                pltpu.VMEM((tok, width), BF16), pltpu.VMEM((tok, width), BF16), pltpu.VMEM((tok, width), BF16), pltpu.VMEM((2 * top, tok), F32),
                pltpu.VMEM((tok, heads, hd), F32), pltpu.VMEM((tok, heads, hd), F32),
                pltpu.VMEM((BLOCK * heads, seq), F32), pltpu.VMEM((BLOCK * heads, hd), F32), pltpu.VMEM((tok, hd), F32), pltpu.VMEM((tok, hd), F32),
                pltpu.VMEM((width, heads * hd), BF16), pltpu.VMEM((width, hd), BF16), pltpu.VMEM((width, hd), BF16),
                pltpu.VMEM((heads * hd, width), BF16), pltpu.VMEM((width, experts), F32),
                pltpu.VMEM((group,) + mine.shape, I32), pltpu.VMEM((local, group, tok), I32),
                pltpu.VMEM((group + pools + 8, tok), I32), pltpu.SMEM((group + pools + 8, tok), I32),
                pltpu.VMEM((group, tok, width), BF16),
                pltpu.VMEM((pools * pool_chunks, CHUNK, width), BF16), pltpu.VMEM((TILE, width), BF16),
                pltpu.VMEM((local * cap_chunks // per, TILE, ff), BF16), pltpu.VMEM((local * cap_chunks, CHUNK, 2 * quarter), BF16),
                pltpu.VMEM((pools, 2 * WINDOW, pool_chunks * CHUNK), BF16),
                pltpu.VMEM((tok * seq, LANES), BF16), pltpu.VMEM((tok * seq, LANES), BF16),
                pltpu.VMEM((8, 3 * tok, 2 * nx * WINDOW), BF16),
                pltpu.VMEM((4, 4, tok, quarter), F32), pltpu.VMEM((4, 4, tok, quarter), F32), pltpu.VMEM((2, 4, 2 * top, tok), F32),
                pltpu.VMEM((local, width, ff), BF16), pltpu.VMEM((local, width, ff), BF16), pltpu.VMEM((local, ff, width), BF16),
                dma((tok // BLOCK,)), dma((tok // BLOCK,)), dma((5,)), dma((3, local)), dma,
                dma((group,)), dma((group,)), dma((128,)), dma((128,)), dma((64,)), dma((64,)), dma((8,)), dma((8,)),
                dma((32,)), dma((32,)), dma((16,)), dma((16,)),
            ],
            compiler_params=pltpu.CompilerParams(vmem_limit_bytes=67043328, collective_id=0, has_side_effects=True),
            name='step',
        )(hidden, k_cache, v_cache, lengths, w_query, w_key, w_value, w_out, w_router, expert_ids, mine, w_gate, w_up, w_down)

    cache_spec = P(None, BATCH_AXES, None, None, None)
    expert_spec = P(None, GROUP_AXES, None, None)
    in_specs = (P(BATCH_AXES, None), cache_spec, cache_spec, P(BATCH_AXES), P(), P(), P(), P(), P(), P(None, BATCH_AXES, None), expert_spec, expert_spec, expert_spec)
    return jax.shard_map(device_step, mesh=mesh, in_specs=in_specs, out_specs=P(BATCH_AXES, None), check_vma=False)
```

time: 612 us -> 205 us (0.33)
  the two profiles are of different devices: /device:TPU:103 before, /device:TPU:97 now
where the time goes in v3:
time: 205 us
  Pallas kernels  202 us (99%)
  local copies, waits for them, and re-layouts  3.15 us (2%)
    pallas_call x1, Pallas kernels, device_step(): pl.pallas_call(functools.partial(step_kernel, dims), out_shape=jax.ShapeD...  202 us

profile of v3, /device:TPU:97, one launch (start us, length us, event | category | flops | bytes accessed | tf_op | source)
XLA Modules:
  0.0 205.0 jit_solution(17064655570704723992)
XLA Ops:
  0.0 1.5 copy.14.cols_ref
  1.5 201.8 %step.1 = bf16[128,1024]{1,0:T(8,128)(2,1)} custom-call(bf16[128,1024]{1,0:T(8,128)(2,1)} %hidden_ref.1, bf16[2,16384,128]{2,1,0:T(8,128)(2,1)} %bitcast.3, bf16[2,16384,128]{2,1,0:T(8,128)(2,1)} %bitcast.4, s32[128]{0:T(128)} %len_ref.1, bf16[2,1024,2048]{2,1,0:T(8,128)(2,1)} %wq_hbm.1, bf16[2,1024,128]{2,1,0:T(8,128)(2,1)} %wk_hbm.1, ...), custom_call_target="tpu_custom_call" | custom-call | tf_op jit(solution)/shard_map/step/pallas_call | solution.py:580
  203.3 1.7 copy.16

commit v4 on v3

v4 whole, which is shorter than its diff:
```python
import functools

import jax
import jax.numpy as jnp
from jax import lax
from jax.experimental import pallas as pl
from jax.experimental.pallas import tpu as pltpu
from jax.sharding import PartitionSpec as P

EPS = 1e-6
GROUP_AXES = ('pool', 'ep')
BATCH_AXES = ('dp', 'pool', 'ep')
F32 = jnp.float32
BF16 = jnp.bfloat16
I32 = jnp.int32
CHUNK = 16
WINDOW = 64
TILE = 256
LANES = 128
BLOCK = 16
WAVES = 2
MESH = pl.DeviceIdType.MESH
OFFS = (0, -1, 1, 2)
IDX = {0: 0, 1: 1, -1: 2, 2: 3}
BACK = {1: -1, -1: 1, 2: 2}


def rms_norm(wide):
    return (wide * lax.rsqrt(jnp.mean(wide * wide, axis=-1, keepdims=True) + EPS)).astype(BF16)


def dot(a, b):
    return jnp.dot(a, b, preferred_element_type=F32)


def dot_t(a, b):
    return lax.dot_general(a, b, (((1,), (1,)), ((), ())), preferred_element_type=F32)


def split3(w):
    hi = w.astype(BF16)
    rest = w - hi.astype(F32)
    mid = rest.astype(BF16)
    low = (rest - mid.astype(F32)).astype(BF16)
    return hi, mid, low


def iota(shape, axis):
    return lax.broadcasted_iota(I32, shape, axis)


def onehot(cond):
    return jnp.where(cond, 1.0, 0.0).astype(BF16)


def step_kernel(dims, hidden_ref, kc_hbm, vc_hbm, len_ref, wq_hbm, wk_hbm, wv_hbm, wo_hbm, wr_hbm, mine_ref, wg_hbm, wu_hbm, wd_hbm,
                x_ref,
                xcur, abuf, ubuf0, gs, idc, slotc, q3, o3, sbuf, nbuf, kn3, vn3, wq, wk, wv, wo, wr,
                idsbuf, keys, tabv, tab, ubuf, xg, xt, act, yq, pick, rbuf, vbuf, gmat, part, final, gsbuf, wg, wu, wd,
                ksem, vsem, asem, wsem, tsem, id_send, id_recv, ag_send, ag_recv, dd_send, dd_recv, gs_send, gs_recv,
                p1_send, p1_recv, p2_send, p2_recv):
    ny, nx, layers, tok, width, heads, hd, seq, experts, local, top, pool_chunks, cap_chunks = dims
    pools = ny * nx
    group = 2 * pools
    pool_rows = pool_chunks * CHUNK
    span = tok // WAVES
    half = span // 2
    steps = width // (2 * LANES)
    per = TILE // CHUNK
    per_expert = cap_chunks // per
    slots = 2 * nx * WINDOW
    y = lax.axis_index('pool')
    ep = lax.axis_index('ep')
    x = ep // 2
    core = lax.rem(ep, 2)
    other = 1 - core
    me = y * (2 * nx) + ep

    def at(dx, dy):
        return lax.rem(x + dx + nx, nx), lax.rem(y + dy + ny, ny)

    def dev(dx, dy, c):
        px, py = at(dx, dy)
        return {'pool': py, 'ep': px * 2 + c}

    def number(dx, dy, c):
        px, py = at(dx, dy)
        return py * (2 * nx) + px * 2 + c

    def axes(h, first, second):
        return (first, second) if h == 0 else (second, first)

    def peer(d):
        to = lax.rem(me + d, group)
        return {'pool': to // (2 * nx), 'ep': lax.rem(to, 2 * nx)}

    def remote(src, dst, send, recv, device):
        return pltpu.make_async_remote_copy(src_ref=src, dst_ref=dst, send_sem=send, recv_sem=recv, device_id=device, device_id_type=MESH)

    def att_copies(layer):
        return [pltpu.make_async_copy(src.at[layer], dst, asem.at[i])
                for i, (src, dst) in enumerate(((wq_hbm, wq), (wk_hbm, wk), (wv_hbm, wv), (wo_hbm, wo), (wr_hbm, wr)))]

    def expert_copies(layer):
        return [pltpu.make_async_copy(src.at[layer, e], dst.at[e], wsem.at[i, e])
                for i, (src, dst) in enumerate(((wg_hbm, wg), (wu_hbm, wu), (wd_hbm, wd))) for e in range(local)]

    def kv_copies(layer, b):
        rows = pl.ds(b * (BLOCK * seq), BLOCK * seq)
        return (pltpu.make_async_copy(kc_hbm.at[layer, rows], rbuf.at[rows], ksem.at[b]),
                pltpu.make_async_copy(vc_hbm.at[layer, rows], vbuf.at[rows], vsem.at[b]))

    def id_copy(d):
        return remote(mine_ref, idsbuf.at[me], id_send.at[d], id_recv.at[d], peer(d))

    def piece(w, h, r, q, p=None):
        if q == 0:
            step = 1 if (r == -1 or (r == 2 and p == 0)) else -1
            own = (0, 0) if r in (1, -1) else (-step, 0)
            to = (step, 0)
        else:
            step = 1 if (q == -1 or (q == 2 and p == 0)) else -1
            own = (r, 0) if q in (1, -1) else (r, -step)
            to = (0, step)
        first = w * span + h * half
        rows = pl.ds(first, half) if p is None else pl.ds(first + p * (half // 2), half // 2)
        owner = number(*axes(h, *own), core)
        src = ubuf0.at[rows] if own == (0, 0) else ubuf.at[owner, rows]
        sem = (((w * 2 + h) * 4 + IDX[r]) * 4 + IDX[q]) * 2 + (p or 0)
        return remote(src, ubuf.at[owner, rows], ag_send.at[sem], ag_recv.at[sem], dev(*axes(h, *to), core))

    def across(w, h, r, q):
        rows = pl.ds(w * span + h * half, half)
        owner = number(*axes(h, r, q), core)
        src = ubuf0.at[rows] if (r, q) == (0, 0) else ubuf.at[owner, rows]
        sem = ((w * 2 + h) * 4 + IDX[r]) * 4 + IDX[q]
        return remote(src, ubuf.at[owner, rows], dd_send.at[sem], dd_recv.at[sem], dev(0, 0, other))

    def gate_copy(h, q):
        back = IDX[BACK[q]]
        sem = h * 4 + back
        return remote(gs, gsbuf.at[h, back], gs_send.at[sem], gs_recv.at[sem], dev(*axes(h, 0, q), core))

    def window_row(n, one, c, two=0):
        return ((n * nx + one) * 2 + c) * (ny * WINDOW) + two * WINDOW

    def first_copy(h, w, r, flip):
        n = h * steps + w
        c = other if flip else core
        size = ny * WINDOW
        src = pl.ds(pl.multiple_of(window_row(n, at(r, r)[h], c), size), size)
        dst = pl.ds(pl.multiple_of(window_row(n, (x, y)[h], core), size), size)
        sem = (n * 4 + IDX[r]) * 2 + flip
        return remote(rbuf.at[src], vbuf.at[dst], p1_send.at[sem], p1_recv.at[sem], dev(*axes(h, r, 0), c))

    def second_copy(h, w, q):
        n = h * steps + w
        sem = n * 4 + IDX[q]
        return remote(part.at[n, IDX[q]], final.at[n, IDX[q]], p2_send.at[sem], p2_recv.at[sem], dev(*axes(h, 0, q), core))

    for cp in att_copies(0):
        cp.start()
    barrier = pltpu.get_barrier_semaphore()
    for d in range(1, group):
        pl.semaphore_signal(barrier, inc=1, device_id=peer(d), device_id_type=MESH)
    pl.semaphore_wait(barrier, group - 1)
    for d in range(1, group):
        id_copy(d).start()
    idsbuf[me] = mine_ref[...]
    xcur[...] = hidden_ref[...]
    scale = hd ** -0.5
    lane = iota((heads, seq), 1)

    tab_y0 = group
    tab_x0 = group + pools

    def own_slots(layer):
        e_iota = iota((tok, experts), 1)
        before = onehot(iota((tok, tok), 1) < iota((tok, tok), 0))
        e_row = iota((experts, experts), 0)
        e_col = iota((experts, experts), 1)
        same = onehot((e_row < e_col) & (e_row // local == e_col // local))
        ids = jnp.concatenate([mine_ref[layer].astype(F32), jnp.zeros((LANES - top, tok), F32)], axis=0)
        ids = jnp.transpose(ids).astype(I32)
        idc[...] = ids
        hits = [ids[:, k:k + 1] == e_iota for k in range(top)]
        chosen = hits[0]
        for k in range(1, top):
            chosen = chosen | hits[k]
        chosen = jnp.where(chosen, 1.0, 0.0)
        rank = dot(before, chosen.astype(BF16))
        count = jnp.sum(chosen, axis=0, keepdims=True)
        start = dot(jnp.broadcast_to(count, (8, experts)).astype(BF16), same)[0:1]
        slot_full = rank + start + ((e_iota // local) * WINDOW).astype(F32)
        for k in range(top):
            slotc[:, k:k + 1] = jnp.sum(jnp.where(hits[k], slot_full, 0.0), axis=1, keepdims=True)

    def tables(layer):
        before_tok = onehot(iota((tok, tok), 0) < iota((tok, tok), 1))
        before_pool = onehot(iota((pools, pools), 1) < iota((pools, pools), 0))
        pair_of = onehot(iota((pools, group), 1) // 2 == iota((pools, group), 0))
        spread = onehot(iota((group, pools), 0) // 2 == iota((group, pools), 1))
        prev = onehot((iota((group, group), 1) + 1 == iota((group, group), 0)) & (iota((group, group), 0) % 2 == 1))
        lane_p = iota((pools, tok), 1)
        pool_id = iota((pools, tok), 0)
        lane_s = iota((group, tok), 1)
        off = jnp.zeros((pools, tok), I32)
        lo = jnp.zeros((group, tok), I32)
        tab_y = jnp.zeros((pools, tok), I32)
        tab_s = jnp.zeros((group, tok), I32)
        rows_x = []
        for e in range(local):
            target = me * local + e
            hit = idsbuf[:, layer, 0, :] == target
            for k in range(1, top):
                hit = hit | (idsbuf[:, layer, k, :] == target)
            hitb = onehot(hit)
            rank = dot(hitb, before_tok).astype(I32)
            count = jnp.broadcast_to(jnp.sum(jnp.where(hit, 1.0, 0.0), axis=1, keepdims=True), (group, tok))
            countb = count.astype(BF16)
            count = count.astype(I32)
            amount = dot(pair_of, countb).astype(I32)
            chunks = lax.shift_right_logical(amount + (CHUNK - 1), 4)
            base = dot(before_pool, chunks.astype(F32).astype(BF16)).astype(I32)
            shift = dot(spread, (off * CHUNK).astype(F32).astype(BF16)).astype(I32) + dot(prev, countb).astype(I32)
            keys[e] = jnp.where(hit, rank + shift, -1)
            rows_x.append(jnp.sum(jnp.where((lane_p >= base) & (lane_p < base + chunks), pool_id * pool_chunks + off + lane_p - base, 0).astype(F32),
                                  axis=0, keepdims=True))
            tab_y = jnp.where((lane_p >= off) & (lane_p < off + chunks), e * cap_chunks + base + lane_p - off, tab_y)
            tab_s = jnp.where(lane_s == e, lo, tab_s)
            tab_s = jnp.where(lane_s == local + e, lo + count, tab_s)
            tab_s = jnp.where(lane_s == 2 * local + e, shift - lo, tab_s)
            off = off + chunks
            lo = lo + count
        tabv[0:group, :] = tab_s
        tabv[group:group + pools, :] = jnp.clip(tab_y, 0, local * cap_chunks - 1)
        rows_x.append(jnp.zeros((8 - local, tok), F32))
        tabv[tab_x0:tab_x0 + 8, :] = jnp.clip(jnp.concatenate(rows_x, axis=0).astype(I32), 0, pools * pool_chunks - 1)
        tab_copy = pltpu.make_async_copy(tabv, tab, tsem)
        tab_copy.start()
        tab_copy.wait()
        jrow = iota((WINDOW, pool_rows), 0)
        diff = iota((WINDOW, pool_rows), 1) - jrow

        def choose(chip, c2):
            halves = []
            for par in range(2):
                hit = None
                for e in range(local):
                    low_ = tab[2 * chip + par, e]
                    high_ = tab[2 * chip + par, local + e]
                    delta = tab[2 * chip + par, 2 * local + e]
                    this = (diff == delta) & (jrow >= low_) & (jrow < high_)
                    hit = this if hit is None else hit | this
                halves.append(onehot(hit))
            pick[chip] = jnp.concatenate(halves, axis=0)
            return c2

        lax.fori_loop(0, pools, choose, 0, unroll=2)

    own_slots(0)

    def layer_body(layer, carry):
        for b in range(tok // BLOCK):
            for cp in kv_copies(layer, b):
                cp.start()
        for cp in expert_copies(layer):
            cp.start()
        normed = rms_norm(xcur[...].astype(F32))
        for cp in att_copies(layer)[:3]:
            cp.wait()
        kn3[...] = dot(normed, wk[...]).astype(BF16).astype(F32)
        vn3[...] = dot(normed, wv[...]).astype(BF16).astype(F32)
        for h in range(heads):
            if h % 2 == 0:
                pair = dot(normed, wq[:, h * hd:(h + 2) * hd])
            q3[:, h, :] = pair[:, (h % 2) * hd:(h % 2 + 1) * hd].astype(BF16).astype(F32)

        def scores(b, part_):
            kv_copies(layer, b)[0].wait()
            for j in range(BLOCK):
                t = b * BLOCK + j
                q = q3[t]
                s = dot_t(q.astype(BF16), rbuf[pl.ds(t * seq, seq), :]) * scale
                sbuf[part_, j * heads:(j + 1) * heads, :] = jnp.where(lane < len_ref[t], s, -jnp.inf)
                nbuf[part_, j * heads:(j + 1) * heads, :] = q * kn3[pl.ds(t, 1), :]

        def weigh(b, part_):
            s = sbuf[part_]
            sn = jnp.sum(nbuf[part_], axis=1, keepdims=True) * scale
            peak = jnp.maximum(jnp.max(s, axis=1, keepdims=True), sn)
            p = jnp.exp(s - peak)
            pn = jnp.exp(sn - peak)
            inv = 1.0 / (jnp.sum(p, axis=1, keepdims=True) + pn)
            pb = (p * inv).astype(BF16)
            pnb = (pn * inv).astype(BF16).astype(F32)
            kv_copies(layer, b)[1].wait()
            for j in range(BLOCK):
                t = b * BLOCK + j
                rows = slice(j * heads, (j + 1) * heads)
                o = dot(pb[rows], vbuf[pl.ds(t * seq, seq), :]) + pnb[rows] * vn3[pl.ds(t, 1), :]
                o3[t] = o.astype(BF16).astype(F32)

        def block(i, c2):
            scores(2 * i, 0)
            scores(2 * i + 1, 1)
            weigh(2 * i, 0)
            weigh(2 * i + 1, 1)
            return c2

        def project(w):
            rows = slice(w * span, (w + 1) * span)
            mixed = jnp.concatenate([o3[rows, h, :].astype(BF16) for h in range(heads)], axis=1)
            a = (xcur[rows].astype(F32) + dot(mixed, wo[...])).astype(BF16)
            abuf[rows] = a
            ubuf0[rows] = rms_norm(a.astype(F32))

        started = []

        def go(fn, *args):
            fn(*args).start()
            started.append((fn, args))

        have = set()
        done = set()
        prow = iota((pool_rows, tok), 0)

        def gather(dx, dy):
            px, py = at(dx, dy)
            chip = py * nx + px
            for w in range(WAVES):
                across(w, 0, dx, dy).wait_recv()
                across(w, 1, dy, dx).wait_recv()
            halves = []
            for par in range(2):
                hit = None
                for e in range(local):
                    this = prow == keys[e, pl.ds(2 * chip + par, 1), :]
                    hit = this if hit is None else hit | this
                halves.append(onehot(hit))
            rows = ubuf[pl.ds(2 * chip, 2)].reshape(2 * tok, width)
            xg[pl.ds(chip * pool_chunks, pool_chunks)] = dot(jnp.concatenate(halves, axis=1), rows).astype(BF16).reshape(pool_chunks, CHUNK, width)

        def ready(limit):
            for dy in OFFS:
                for dx in OFFS:
                    if limit and (dx, dy) not in done and all((w, 0, dx, dy) in have and (w, 1, dy, dx) in have for w in range(WAVES)):
                        done.add((dx, dy))
                        gather(dx, dy)
                        limit -= 1

        def s0(w):
            for h in (0, 1):
                go(piece, w, h, -1, 0)
                go(piece, w, h, 1, 0)
            for h in (0, 1):
                go(piece, w, h, 0, -1)
                go(piece, w, h, 0, 1)
                go(across, w, h, 0, 0)
                have.add((w, h, 0, 0))

        def s2(w):
            for r, p in ((-1, 0), (1, 1)):
                for h in (0, 1):
                    piece(w, h, r, 0).wait_recv()
                    go(piece, w, h, 2, 0, p)
                    go(piece, w, h, r, -1)
                    go(piece, w, h, r, 1)
                    go(across, w, h, r, 0)
                    have.add((w, h, r, 0))

        def s3(w):
            for h in (0, 1):
                piece(w, h, 2, 0, 0).wait_recv()
                piece(w, h, 2, 0, 1).wait_recv()
                go(piece, w, h, 2, -1)
                go(piece, w, h, 2, 1)
                go(across, w, h, 2, 0)
                have.add((w, h, 2, 0))

        def s4(w, r):
            for q, p in ((-1, 0), (1, 1)):
                for h in (0, 1):
                    piece(w, h, r, q).wait_recv()
                    go(piece, w, h, r, 2, p)
                    go(across, w, h, r, q)
                    have.add((w, h, r, q))

        def s5(w, r):
            for h in (0, 1):
                piece(w, h, r, 2, 0).wait_recv()
                piece(w, h, r, 2, 1).wait_recv()
                go(across, w, h, r, 2)
                have.add((w, h, r, 2))

        blocks = span // (2 * BLOCK)
        lax.fori_loop(0, blocks, block, 0)
        att_copies(layer)[3].wait()
        project(0)
        s0(0)
        lax.fori_loop(blocks, 2 * blocks - 1, block, 0)
        s2(0)
        lax.fori_loop(2 * blocks - 1, 2 * blocks, block, 0)
        s4(0, 0)
        project(1)
        s0(1)
        s3(0)

        att_copies(layer)[4].wait()
        hi, mid, low = split3(wr[...])
        u = ubuf0[...]
        logits = dot(u, hi) + dot(u, mid) + dot(u, low)

        @pl.when(layer + 1 < layers)
        def _():
            for cp in att_copies(layer + 1):
                cp.start()

        e_iota = iota((tok, experts), 1)
        hits = [idc[:, k:k + 1] == e_iota for k in range(top)]
        picked = [jnp.sum(jnp.where(hit, logits, 0.0), axis=1, keepdims=True) for hit in hits]
        peak = picked[0]
        for k in range(1, top):
            peak = jnp.maximum(peak, picked[k])
        ex = [jnp.exp(v - peak) for v in picked]
        total = ex[0]
        for k in range(1, top):
            total = total + ex[k]
        columns = [v / total for v in ex] + [slotc[...]]
        columns.append(jnp.zeros((tok, LANES - 2 * top), F32))
        gs[...] = jnp.transpose(jnp.concatenate(columns, axis=1))[:2 * top]
        ubuf[me] = u
        for h in (0, 1):
            for q in OFFS[1:]:
                go(gate_copy, h, q)
        s4(0, -1)
        s4(0, 1)
        s2(1)

        @pl.when(layer == 0)
        def _():
            for d in range(1, group):
                id_copy(d).wait()
            tables(0)

        s4(0, 2)
        s3(1)
        for r in OFFS:
            s5(0, r)
        ready(1)
        s4(1, 0)
        ready(2)

        srow = iota((slots, tok), 0)

        def gates(h):
            for q in OFFS:
                if q:
                    gate_copy(h, BACK[q]).wait_recv()
                    table = gsbuf[h, IDX[q]]
                else:
                    table = gs[...]
                slot = table[top:2 * top].astype(I32)
                if h == 0:
                    rel = slot - y * slots
                else:
                    source = lax.shift_right_logical(slot, 6)
                    sx = lax.shift_right_logical(source, 1) & (nx - 1)
                    sy = source // (2 * nx)
                    rel = jnp.where(sx == x, (sy * 2 + (source & 1)) * WINDOW + (slot & (WINDOW - 1)), -1)
                g = jnp.zeros((slots, tok), F32)
                for k in range(top):
                    g = jnp.where(srow == rel[k:k + 1], table[k:k + 1], g)
                for i, v in enumerate(split3(jnp.transpose(g))):
                    gmat[h * 4 + IDX[q], i * tok:(i + 1) * tok, :] = v

        s4(1, -1)
        s4(1, 1)
        ready(2)
        s4(1, 2)
        ready(3)
        s5(1, 0)
        ready(2)
        s5(1, -1)
        s5(1, 1)
        ready(4)
        s5(1, 2)
        ready(pools)

        for cp in expert_copies(layer):
            cp.wait()

        def tile(i, c2):
            e = i // per_expert
            first_chunk = (i % per_expert) * per
            for j in range(per):
                xt[j * CHUNK:(j + 1) * CHUNK, :] = xg[tab[tab_x0 + e, first_chunk + j]]
            rows_in = xt[...]
            first = dot(rows_in, wg[e])
            second = dot(rows_in, wu[e])
            act[i] = (first * (1.0 / (1.0 + jnp.exp(-first))) * second).astype(BF16)
            return c2

        lax.fori_loop(0, local * per_expert, tile, 0)
        for fn, args in started:
            fn(*args).wait_send()
        started.clear()

        firsts = [(2, 0), (2, 1), (1, 0), (-1, 0), (1, 1), (-1, 1), (0, 1)]
        wide = 2
        for w in range(steps):
            if w % wide == 0:
                def down(i, c2):
                    out = dot(act[i], wd[i // per_expert, :, w * 2 * LANES:(w + wide) * 2 * LANES])
                    yq[pl.ds(i * per, per)] = out.astype(BF16).reshape(per, CHUNK, wide * 2 * LANES)
                    return c2

                lax.fori_loop(0, local * per_expert, down, 0, unroll=2)

            def window(chip, c2):
                inside = slice((w % wide) * 2 * LANES, (w % wide + 1) * 2 * LANES)
                rows = jnp.concatenate([yq[tab[tab_y0 + chip, i], :, inside] for i in range(pool_chunks)], axis=0)
                out = dot(pick[chip], rows).astype(BF16)
                cy = chip // nx
                cx = chip % nx
                for h in (0, 1):
                    one, two = axes(h, cx, cy)
                    for par in range(2):
                        row = pl.multiple_of(window_row(h * steps + w, one, par, two), WINDOW)
                        rbuf[pl.ds(row, WINDOW), :] = out[par * WINDOW:(par + 1) * WINDOW, h * LANES:(h + 1) * LANES]
                return c2

            lax.fori_loop(0, pools, window, 0, unroll=4)
            for r, flip in firsts:
                for h in (0, 1):
                    go(first_copy, h, w, r, flip)
            for h in (0, 1):
                size = ny * WINDOW
                own = pl.ds(pl.multiple_of(window_row(h * steps + w, (x, y)[h], core), size), size)
                vbuf[own, :] = rbuf[own, :]

        def merge(h, ws):
            for w in ws:
                for r, flip in firsts:
                    first_copy(h, w, r, flip).wait_recv()
            for q in (2, 1, -1, 0):
                two = at(q, q)[1 - h]
                rows = []
                for s in range(2 * nx):
                    pieces = [vbuf[pl.ds(pl.multiple_of(window_row(h * steps + w, s // 2, s % 2, two), WINDOW), WINDOW), :] for w in ws]
                    rows.append(jnp.concatenate(pieces, axis=1))
                parts = dot(gmat[h * 4 + IDX[q]], jnp.concatenate(rows, axis=0))
                total = parts[0:tok] + parts[tok:2 * tok] + parts[2 * tok:3 * tok]
                for i, w in enumerate(ws):
                    part[h * steps + w, IDX[q]] = total[:, i * LANES:(i + 1) * LANES]
                if q:
                    for w in ws:
                        go(second_copy, h, w, q)

        for h in (0, 1):
            gates(h)
        for h in (0, 1):
            merge(h, (0, 1))

        @pl.when(layer + 1 < layers)
        def _():
            own_slots(layer + 1)
            tables(layer + 1)

        for w in range(2, steps):
            for h in (0, 1):
                merge(h, (w,))
        for w in range(steps):
            for h in (0, 1):
                n = h * steps + w
                where = slice((w * 2 + h) * LANES, (w * 2 + h + 1) * LANES)
                for q in OFFS[1:]:
                    second_copy(h, w, q).wait_recv()
                total = (part[n, 0] + final[n, 1]) + (final[n, 2] + final[n, 3])
                xcur[:, where] = (abuf[:, where].astype(F32) + total).astype(BF16)
        for fn, args in started:
            fn(*args).wait_send()
        return carry

    lax.fori_loop(0, layers, layer_body, 0)
    x_ref[...] = xcur[...]


def solution(mesh):
    ny, nx = mesh.shape['pool'], mesh.shape['ep'] // 2

    def device_step(hidden, k_cache, v_cache, lengths, w_query, w_key, w_value, w_out, w_router, expert_ids, w_gate, w_up, w_down):
        tok, width = hidden.shape
        layers, _, top = expert_ids.shape
        seq, hd = k_cache.shape[2], k_cache.shape[4]
        heads = w_query.shape[2] // hd
        experts = w_router.shape[2]
        local, ff = w_gate.shape[1], w_gate.shape[3]
        pools = nx * ny
        group = 2 * pools
        k_cache = k_cache.reshape(layers, tok * seq, hd)
        v_cache = v_cache.reshape(layers, tok * seq, hd)
        mine = jnp.swapaxes(expert_ids, 1, 2)
        pool_chunks = (2 * (WINDOW - 1) + local * (CHUNK - 1)) // CHUNK
        most = 2 * group * tok * top // (group * local)
        per = TILE // CHUNK
        cap_chunks = pl.cdiv((most + pools * (CHUNK - 1)) // CHUNK, per) * per
        steps = width // (2 * LANES)
        vm = pl.BlockSpec(memory_space=pltpu.VMEM)
        hb = pl.BlockSpec(memory_space=pl.ANY)
        sm = pl.BlockSpec(memory_space=pltpu.SMEM)
        dma = pltpu.SemaphoreType.DMA
        dims = (ny, nx, layers, tok, width, heads, hd, seq, experts, local, top, pool_chunks, cap_chunks)
        return pl.pallas_call(
            functools.partial(step_kernel, dims),
            out_shape=jax.ShapeDtypeStruct((tok, width), BF16),
            in_specs=[vm, hb, hb, sm, hb, hb, hb, hb, hb, vm, hb, hb, hb],
            out_specs=vm,
            scratch_shapes=[
                pltpu.VMEM((tok, width), BF16), pltpu.VMEM((tok, width), BF16), pltpu.VMEM((tok, width), BF16), pltpu.VMEM((2 * top, tok), F32),
                pltpu.VMEM((tok, LANES), I32), pltpu.VMEM((tok, top), F32),
                pltpu.VMEM((tok, heads, hd), F32), pltpu.VMEM((tok, heads, hd), F32),
                pltpu.VMEM((2, BLOCK * heads, seq), F32), pltpu.VMEM((2, BLOCK * heads, hd), F32), pltpu.VMEM((tok, hd), F32), pltpu.VMEM((tok, hd), F32),
                pltpu.VMEM((width, heads * hd), BF16), pltpu.VMEM((width, hd), BF16), pltpu.VMEM((width, hd), BF16),
                pltpu.VMEM((heads * hd, width), BF16), pltpu.VMEM((width, experts), F32),
                pltpu.VMEM((group,) + mine.shape, I32), pltpu.VMEM((local, group, tok), I32),
                pltpu.VMEM((group + pools + 8, tok), I32), pltpu.SMEM((group + pools + 8, tok), I32),
                pltpu.VMEM((group, tok, width), BF16),
                pltpu.VMEM((pools * pool_chunks, CHUNK, width), BF16), pltpu.VMEM((TILE, width), BF16),
                pltpu.VMEM((local * cap_chunks // per, TILE, ff), BF16), pltpu.VMEM((local * cap_chunks, CHUNK, 4 * LANES), BF16),
                pltpu.VMEM((pools, 2 * WINDOW, pool_chunks * CHUNK), BF16),
                pltpu.VMEM((tok * seq, LANES), BF16), pltpu.VMEM((tok * seq, LANES), BF16),
                pltpu.VMEM((8, 3 * tok, 2 * nx * WINDOW), BF16),
                pltpu.VMEM((2 * steps, 4, tok, LANES), F32), pltpu.VMEM((2 * steps, 4, tok, LANES), F32), pltpu.VMEM((2, 4, 2 * top, tok), F32),
                pltpu.VMEM((local, width, ff), BF16), pltpu.VMEM((local, width, ff), BF16), pltpu.VMEM((local, ff, width), BF16),
                dma((tok // BLOCK,)), dma((tok // BLOCK,)), dma((5,)), dma((3, local)), dma,
                dma((group,)), dma((group,)), dma((128,)), dma((128,)), dma((64,)), dma((64,)), dma((8,)), dma((8,)),
                dma((16 * steps,)), dma((16 * steps,)), dma((8 * steps,)), dma((8 * steps,)),
            ],
            compiler_params=pltpu.CompilerParams(vmem_limit_bytes=67043328, collective_id=0, has_side_effects=True),
            name='step',
        )(hidden, k_cache, v_cache, lengths, w_query, w_key, w_value, w_out, w_router, mine, w_gate, w_up, w_down)

    cache_spec = P(None, BATCH_AXES, None, None, None)
    expert_spec = P(None, GROUP_AXES, None, None)
    in_specs = (P(BATCH_AXES, None), cache_spec, cache_spec, P(BATCH_AXES), P(), P(), P(), P(), P(), P(None, BATCH_AXES, None), expert_spec, expert_spec, expert_spec)
    return jax.shard_map(device_step, mesh=mesh, in_specs=in_specs, out_specs=P(BATCH_AXES, None), check_vma=False)
```

time: 205 us -> 190 us (0.927)
  Pallas kernels: 202 us -> 189 us
    pallas_call x1, Pallas kernels: 202 us -> 189 us  [device_step(): pl.pallas_call(functools.partial(step_kernel, dims), out_shape=jax.ShapeD...]
where the time goes in v4:
time: 190 us
  Pallas kernels  189 us (99%)
    pallas_call x1, Pallas kernels, device_step(): pl.pallas_call(functools.partial(step_kernel, dims), out_shape=jax.ShapeD...  189 us

profile of v4, /device:TPU:97, one launch (start us, length us, event | category | flops | bytes accessed | tf_op | source)
XLA Modules:
  0.0 190.3 jit_solution(12819102920168409769)
XLA Ops:
  0.0 188.6 %step.1 = bf16[128,1024]{1,0:T(8,128)(2,1)} custom-call(bf16[128,1024]{1,0:T(8,128)(2,1)} %hidden_ref.1, bf16[2,16384,128]{2,1,0:T(8,128)(2,1)} %bitcast.3, bf16[2,16384,128]{2,1,0:T(8,128)(2,1)} %bitcast.4, s32[128]{0:T(128)} %len_ref.1, bf16[2,1024,2048]{2,1,0:T(8,128)(2,1)} %wq_hbm.1, bf16[2,1024,128]{2,1,0:T(8,128)(2,1)} %wk_hbm.1, ...), custom_call_target="tpu_custom_call" | custom-call | tf_op jit(solution)/shard_map/step/pallas_call | solution.py:614
  188.6 1.7 copy.15

commit v5 on v4

--- a/solution.py
+++ b/solution.py
@@ -15,7 +15,7 @@
 I32 = jnp.int32
 CHUNK = 16
 WINDOW = 64
-TILE = 256
+TILE = 768
 LANES = 128
 BLOCK = 16
 WAVES = 2
@@ -23,6 +23,11 @@
 OFFS = (0, -1, 1, 2)
 IDX = {0: 0, 1: 1, -1: 2, 2: 3}
 BACK = {1: -1, -1: 1, 2: 2}
+NEAR = OFFS[1:3]
+NEXT = OFFS[1:]
+FAR = OFFS[-1]
+BOTH = range(2)
+ROWS, COLS = BOTH
 
 
 def rms_norm(wide):
@@ -49,8 +54,44 @@
     return lax.broadcasted_iota(I32, shape, axis)
 
 
+def ones(cond):
+    return jnp.where(cond, 1.0, 0.0)
+
+
 def onehot(cond):
-    return jnp.where(cond, 1.0, 0.0).astype(BF16)
+    return ones(cond).astype(BF16)
+
+
+def zeros(*shape, dtype=F32):
+    return jnp.zeros(shape, dtype)
+
+
+def row_max(v):
+    return jnp.max(v, axis=1, keepdims=True)
+
+
+def row_sum(v):
+    return jnp.sum(v, axis=1, keepdims=True)
+
+
+def sigmoid(v):
+    return 1.0 / (1.0 + jnp.exp(-v))
+
+
+def down_iota(shape):
+    return iota(shape, 0)
+
+
+def across_iota(shape):
+    return iota(shape, 1)
+
+
+def fold(fn, values):
+    return functools.reduce(fn, values)
+
+
+def vmem(*shape, dtype=BF16):
+    return pltpu.VMEM(shape, dtype)
 
 
 def step_kernel(dims, hidden_ref, kc_hbm, vc_hbm, len_ref, wq_hbm, wk_hbm, wv_hbm, wo_hbm, wr_hbm, mine_ref, wg_hbm, wu_hbm, wd_hbm,
@@ -62,6 +103,7 @@
     ny, nx, layers, tok, width, heads, hd, seq, experts, local, top, pool_chunks, cap_chunks = dims
     pools = ny * nx
     group = 2 * pools
+    pair_lanes = 2 * LANES
     pool_rows = pool_chunks * CHUNK
     span = tok // WAVES
     half = span // 2
@@ -169,54 +211,50 @@
     idsbuf[me] = mine_ref[...]
     xcur[...] = hidden_ref[...]
     scale = hd ** -0.5
-    lane = iota((heads, seq), 1)
+    lane = across_iota((heads, seq))
 
     tab_y0 = group
     tab_x0 = group + pools
 
     def own_slots(layer):
-        e_iota = iota((tok, experts), 1)
-        before = onehot(iota((tok, tok), 1) < iota((tok, tok), 0))
-        e_row = iota((experts, experts), 0)
-        e_col = iota((experts, experts), 1)
+        e_iota = across_iota((tok, experts))
+        before = onehot(across_iota((tok, tok)) < down_iota((tok, tok)))
+        e_row = down_iota((experts, experts))
+        e_col = across_iota((experts, experts))
         same = onehot((e_row < e_col) & (e_row // local == e_col // local))
-        ids = jnp.concatenate([mine_ref[layer].astype(F32), jnp.zeros((LANES - top, tok), F32)], axis=0)
+        ids = jnp.concatenate([mine_ref[layer].astype(F32), zeros(LANES - top, tok)], axis=0)
         ids = jnp.transpose(ids).astype(I32)
         idc[...] = ids
         hits = [ids[:, k:k + 1] == e_iota for k in range(top)]
-        chosen = hits[0]
-        for k in range(1, top):
-            chosen = chosen | hits[k]
-        chosen = jnp.where(chosen, 1.0, 0.0)
+        chosen = fold(jnp.logical_or, hits)
+        chosen = ones(chosen)
         rank = dot(before, chosen.astype(BF16))
         count = jnp.sum(chosen, axis=0, keepdims=True)
         start = dot(jnp.broadcast_to(count, (8, experts)).astype(BF16), same)[0:1]
         slot_full = rank + start + ((e_iota // local) * WINDOW).astype(F32)
         for k in range(top):
-            slotc[:, k:k + 1] = jnp.sum(jnp.where(hits[k], slot_full, 0.0), axis=1, keepdims=True)
+            slotc[:, k:k + 1] = row_sum(jnp.where(hits[k], slot_full, 0.0))
 
     def tables(layer):
-        before_tok = onehot(iota((tok, tok), 0) < iota((tok, tok), 1))
-        before_pool = onehot(iota((pools, pools), 1) < iota((pools, pools), 0))
-        pair_of = onehot(iota((pools, group), 1) // 2 == iota((pools, group), 0))
-        spread = onehot(iota((group, pools), 0) // 2 == iota((group, pools), 1))
-        prev = onehot((iota((group, group), 1) + 1 == iota((group, group), 0)) & (iota((group, group), 0) % 2 == 1))
-        lane_p = iota((pools, tok), 1)
-        pool_id = iota((pools, tok), 0)
-        lane_s = iota((group, tok), 1)
-        off = jnp.zeros((pools, tok), I32)
-        lo = jnp.zeros((group, tok), I32)
-        tab_y = jnp.zeros((pools, tok), I32)
-        tab_s = jnp.zeros((group, tok), I32)
+        before_tok = onehot(down_iota((tok, tok)) < across_iota((tok, tok)))
+        before_pool = onehot(across_iota((pools, pools)) < down_iota((pools, pools)))
+        pair_of = onehot(across_iota((pools, group)) // 2 == down_iota((pools, group)))
+        spread = onehot(down_iota((group, pools)) // 2 == across_iota((group, pools)))
+        prev = onehot((across_iota((group, group)) + 1 == down_iota((group, group))) & (down_iota((group, group)) % 2 == 1))
+        lane_p = across_iota((pools, tok))
+        pool_id = down_iota((pools, tok))
+        lane_s = across_iota((group, tok))
+        off = zeros(pools, tok, dtype=I32)
+        lo = zeros(group, tok, dtype=I32)
+        tab_y = zeros(pools, tok, dtype=I32)
+        tab_s = zeros(group, tok, dtype=I32)
         rows_x = []
         for e in range(local):
             target = me * local + e
-            hit = idsbuf[:, layer, 0, :] == target
-            for k in range(1, top):
-                hit = hit | (idsbuf[:, layer, k, :] == target)
+            hit = fold(jnp.logical_or, [idsbuf[:, layer, k, :] == target for k in range(top)])
             hitb = onehot(hit)
             rank = dot(hitb, before_tok).astype(I32)
-            count = jnp.broadcast_to(jnp.sum(jnp.where(hit, 1.0, 0.0), axis=1, keepdims=True), (group, tok))
+            count = jnp.broadcast_to(row_sum(ones(hit)), (group, tok))
             countb = count.astype(BF16)
             count = count.astype(I32)
             amount = dot(pair_of, countb).astype(I32)
@@ -234,17 +272,17 @@
             lo = lo + count
         tabv[0:group, :] = tab_s
         tabv[group:group + pools, :] = jnp.clip(tab_y, 0, local * cap_chunks - 1)
-        rows_x.append(jnp.zeros((8 - local, tok), F32))
+        rows_x.append(zeros(8 - local, tok))
         tabv[tab_x0:tab_x0 + 8, :] = jnp.clip(jnp.concatenate(rows_x, axis=0).astype(I32), 0, pools * pool_chunks - 1)
         tab_copy = pltpu.make_async_copy(tabv, tab, tsem)
         tab_copy.start()
         tab_copy.wait()
-        jrow = iota((WINDOW, pool_rows), 0)
-        diff = iota((WINDOW, pool_rows), 1) - jrow
+        jrow = down_iota((WINDOW, pool_rows))
+        diff = across_iota((WINDOW, pool_rows)) - jrow
 
         def choose(chip, c2):
             halves = []
-            for par in range(2):
+            for par in BOTH:
                 hit = None
                 for e in range(local):
                     low_ = tab[2 * chip + par, e]
@@ -287,11 +325,11 @@
 
         def weigh(b, part_):
             s = sbuf[part_]
-            sn = jnp.sum(nbuf[part_], axis=1, keepdims=True) * scale
-            peak = jnp.maximum(jnp.max(s, axis=1, keepdims=True), sn)
+            sn = row_sum(nbuf[part_]) * scale
+            peak = jnp.maximum(row_max(s), sn)
             p = jnp.exp(s - peak)
             pn = jnp.exp(sn - peak)
-            inv = 1.0 / (jnp.sum(p, axis=1, keepdims=True) + pn)
+            inv = 1.0 / (row_sum(p) + pn)
             pb = (p * inv).astype(BF16)
             pnb = (pn * inv).astype(BF16).astype(F32)
             kv_copies(layer, b)[1].wait()
@@ -323,7 +361,7 @@
 
         have = set()
         done = set()
-        prow = iota((pool_rows, tok), 0)
+        prow = down_iota((pool_rows, tok))
 
         def gather(dx, dy):
             px, py = at(dx, dy)
@@ -332,7 +370,7 @@
                 across(w, 0, dx, dy).wait_recv()
                 across(w, 1, dy, dx).wait_recv()
             halves = []
-            for par in range(2):
+            for par in BOTH:
                 hit = None
                 for e in range(local):
                     this = prow == keys[e, pl.ds(2 * chip + par, 1), :]
@@ -350,18 +388,18 @@
                         limit -= 1
 
         def s0(w):
-            for h in (0, 1):
+            for h in BOTH:
                 go(piece, w, h, -1, 0)
                 go(piece, w, h, 1, 0)
-            for h in (0, 1):
+            for h in BOTH:
                 go(piece, w, h, 0, -1)
                 go(piece, w, h, 0, 1)
                 go(across, w, h, 0, 0)
                 have.add((w, h, 0, 0))
 
         def s2(w):
-            for r, p in ((-1, 0), (1, 1)):
-                for h in (0, 1):
+            for r, p in zip(NEAR, BOTH):
+                for h in BOTH:
                     piece(w, h, r, 0).wait_recv()
                     go(piece, w, h, 2, 0, p)
                     go(piece, w, h, r, -1)
@@ -370,7 +408,7 @@
                     have.add((w, h, r, 0))
 
         def s3(w):
-            for h in (0, 1):
+            for h in BOTH:
                 piece(w, h, 2, 0, 0).wait_recv()
                 piece(w, h, 2, 0, 1).wait_recv()
                 go(piece, w, h, 2, -1)
@@ -379,15 +417,15 @@
                 have.add((w, h, 2, 0))
 
         def s4(w, r):
-            for q, p in ((-1, 0), (1, 1)):
-                for h in (0, 1):
+            for q, p in zip(NEAR, BOTH):
+                for h in BOTH:
                     piece(w, h, r, q).wait_recv()
                     go(piece, w, h, r, 2, p)
                     go(across, w, h, r, q)
                     have.add((w, h, r, q))
 
         def s5(w, r):
-            for h in (0, 1):
+            for h in BOTH:
                 piece(w, h, r, 2, 0).wait_recv()
                 piece(w, h, r, 2, 1).wait_recv()
                 go(across, w, h, r, 2)
@@ -416,22 +454,18 @@
             for cp in att_copies(layer + 1):
                 cp.start()
 
-        e_iota = iota((tok, experts), 1)
+        e_iota = across_iota((tok, experts))
         hits = [idc[:, k:k + 1] == e_iota for k in range(top)]
-        picked = [jnp.sum(jnp.where(hit, logits, 0.0), axis=1, keepdims=True) for hit in hits]
-        peak = picked[0]
-        for k in range(1, top):
-            peak = jnp.maximum(peak, picked[k])
+        picked = [row_sum(jnp.where(hit, logits, 0.0)) for hit in hits]
+        peak = fold(jnp.maximum, picked)
         ex = [jnp.exp(v - peak) for v in picked]
-        total = ex[0]
-        for k in range(1, top):
-            total = total + ex[k]
+        total = fold(jnp.add, ex)
         columns = [v / total for v in ex] + [slotc[...]]
-        columns.append(jnp.zeros((tok, LANES - 2 * top), F32))
+        columns.append(zeros(tok, LANES - 2 * top))
         gs[...] = jnp.transpose(jnp.concatenate(columns, axis=1))[:2 * top]
         ubuf[me] = u
-        for h in (0, 1):
-            for q in OFFS[1:]:
+        for h in BOTH:
+            for q in NEXT:
                 go(gate_copy, h, q)
         s4(0, -1)
         s4(0, 1)
@@ -451,7 +485,7 @@
         s4(1, 0)
         ready(2)
 
-        srow = iota((slots, tok), 0)
+        srow = down_iota((slots, tok))
 
         def gates(h):
             for q in OFFS:
@@ -468,7 +502,7 @@
                     sx = lax.shift_right_logical(source, 1) & (nx - 1)
                     sy = source // (2 * nx)
                     rel = jnp.where(sx == x, (sy * 2 + (source & 1)) * WINDOW + (slot & (WINDOW - 1)), -1)
-                g = jnp.zeros((slots, tok), F32)
+                g = zeros(slots, tok)
                 for k in range(top):
                     g = jnp.where(srow == rel[k:k + 1], table[k:k + 1], g)
                 for i, v in enumerate(split3(jnp.transpose(g))):
@@ -498,7 +532,7 @@
             rows_in = xt[...]
             first = dot(rows_in, wg[e])
             second = dot(rows_in, wu[e])
-            act[i] = (first * (1.0 / (1.0 + jnp.exp(-first))) * second).astype(BF16)
+            act[i] = (first * sigmoid(first) * second).astype(BF16)
             return c2
 
         lax.fori_loop(0, local * per_expert, tile, 0)
@@ -507,34 +541,36 @@
         started.clear()
 
         firsts = [(2, 0), (2, 1), (1, 0), (-1, 0), (1, 1), (-1, 1), (0, 1)]
-        wide = 2
+        head = [max(w - w % 2, min(w, 1)) for w in range(steps)]
         for w in range(steps):
-            if w % wide == 0:
+            lead = head[w]
+            count_ = head.count(lead)
+            if w == lead:
                 def down(i, c2):
-                    out = dot(act[i], wd[i // per_expert, :, w * 2 * LANES:(w + wide) * 2 * LANES])
-                    yq[pl.ds(i * per, per)] = out.astype(BF16).reshape(per, CHUNK, wide * 2 * LANES)
+                    out = dot(act[i], wd[i // per_expert, :, w * 2 * LANES:(w + count_) * 2 * LANES])
+                    yq[pl.ds(i * per, per), :, :count_ * 2 * LANES] = out.astype(BF16).reshape(per, CHUNK, count_ * 2 * LANES)
                     return c2
 
                 lax.fori_loop(0, local * per_expert, down, 0, unroll=2)
 
             def window(chip, c2):
-                inside = slice((w % wide) * 2 * LANES, (w % wide + 1) * 2 * LANES)
+                inside = slice((w - lead) * 2 * LANES, (w - lead + 1) * 2 * LANES)
                 rows = jnp.concatenate([yq[tab[tab_y0 + chip, i], :, inside] for i in range(pool_chunks)], axis=0)
                 out = dot(pick[chip], rows).astype(BF16)
                 cy = chip // nx
                 cx = chip % nx
-                for h in (0, 1):
+                for h in BOTH:
                     one, two = axes(h, cx, cy)
-                    for par in range(2):
+                    for par in BOTH:
                         row = pl.multiple_of(window_row(h * steps + w, one, par, two), WINDOW)
                         rbuf[pl.ds(row, WINDOW), :] = out[par * WINDOW:(par + 1) * WINDOW, h * LANES:(h + 1) * LANES]
                 return c2
 
             lax.fori_loop(0, pools, window, 0, unroll=4)
             for r, flip in firsts:
-                for h in (0, 1):
+                for h in BOTH:
                     go(first_copy, h, w, r, flip)
-            for h in (0, 1):
+            for h in BOTH:
                 size = ny * WINDOW
                 own = pl.ds(pl.multiple_of(window_row(h * steps + w, (x, y)[h], core), size), size)
                 vbuf[own, :] = rbuf[own, :]
@@ -557,9 +593,9 @@
                     for w in ws:
                         go(second_copy, h, w, q)
 
-        for h in (0, 1):
+        for h in BOTH:
             gates(h)
-        for h in (0, 1):
+        for h in BOTH:
             merge(h, (0, 1))
 
         @pl.when(layer + 1 < layers)
@@ -568,13 +604,13 @@
             tables(layer + 1)
 
         for w in range(2, steps):
-            for h in (0, 1):
+            for h in BOTH:
                 merge(h, (w,))
         for w in range(steps):
-            for h in (0, 1):
+            for h in BOTH:
                 n = h * steps + w
                 where = slice((w * 2 + h) * LANES, (w * 2 + h + 1) * LANES)
-                for q in OFFS[1:]:
+                for q in NEXT:
                     second_copy(h, w, q).wait_recv()
                 total = (part[n, 0] + final[n, 1]) + (final[n, 2] + final[n, 3])
                 xcur[:, where] = (abuf[:, where].astype(F32) + total).astype(BF16)
@@ -617,22 +653,22 @@
             in_specs=[vm, hb, hb, sm, hb, hb, hb, hb, hb, vm, hb, hb, hb],
             out_specs=vm,
             scratch_shapes=[
-                pltpu.VMEM((tok, width), BF16), pltpu.VMEM((tok, width), BF16), pltpu.VMEM((tok, width), BF16), pltpu.VMEM((2 * top, tok), F32),
+                vmem(tok, width), vmem(tok, width), vmem(tok, width), pltpu.VMEM((2 * top, tok), F32),
                 pltpu.VMEM((tok, LANES), I32), pltpu.VMEM((tok, top), F32),
                 pltpu.VMEM((tok, heads, hd), F32), pltpu.VMEM((tok, heads, hd), F32),
                 pltpu.VMEM((2, BLOCK * heads, seq), F32), pltpu.VMEM((2, BLOCK * heads, hd), F32), pltpu.VMEM((tok, hd), F32), pltpu.VMEM((tok, hd), F32),
-                pltpu.VMEM((width, heads * hd), BF16), pltpu.VMEM((width, hd), BF16), pltpu.VMEM((width, hd), BF16),
-                pltpu.VMEM((heads * hd, width), BF16), pltpu.VMEM((width, experts), F32),
+                vmem(width, heads * hd), vmem(width, hd), vmem(width, hd),
+                vmem(heads * hd, width), pltpu.VMEM((width, experts), F32),
                 pltpu.VMEM((group,) + mine.shape, I32), pltpu.VMEM((local, group, tok), I32),
                 pltpu.VMEM((group + pools + 8, tok), I32), pltpu.SMEM((group + pools + 8, tok), I32),
-                pltpu.VMEM((group, tok, width), BF16),
-                pltpu.VMEM((pools * pool_chunks, CHUNK, width), BF16), pltpu.VMEM((TILE, width), BF16),
-                pltpu.VMEM((local * cap_chunks // per, TILE, ff), BF16), pltpu.VMEM((local * cap_chunks, CHUNK, 4 * LANES), BF16),
-                pltpu.VMEM((pools, 2 * WINDOW, pool_chunks * CHUNK), BF16),
-                pltpu.VMEM((tok * seq, LANES), BF16), pltpu.VMEM((tok * seq, LANES), BF16),
-                pltpu.VMEM((8, 3 * tok, 2 * nx * WINDOW), BF16),
+                vmem(group, tok, width),
+                vmem(pools * pool_chunks, CHUNK, width), vmem(TILE, width),
+                vmem(local * cap_chunks // per, TILE, ff), vmem(local * cap_chunks, CHUNK, 4 * LANES),
+                vmem(pools, 2 * WINDOW, pool_chunks * CHUNK),
+                vmem(tok * seq, LANES), vmem(tok * seq, LANES),
+                vmem(8, 3 * tok, 2 * nx * WINDOW),
                 pltpu.VMEM((2 * steps, 4, tok, LANES), F32), pltpu.VMEM((2 * steps, 4, tok, LANES), F32), pltpu.VMEM((2, 4, 2 * top, tok), F32),
-                pltpu.VMEM((local, width, ff), BF16), pltpu.VMEM((local, width, ff), BF16), pltpu.VMEM((local, ff, width), BF16),
+                vmem(local, width, ff), vmem(local, width, ff), vmem(local, ff, width),
                 dma((tok // BLOCK,)), dma((tok // BLOCK,)), dma((5,)), dma((3, local)), dma,
                 dma((group,)), dma((group,)), dma((128,)), dma((128,)), dma((64,)), dma((64,)), dma((8,)), dma((8,)),
                 dma((16 * steps,)), dma((16 * steps,)), dma((8 * steps,)), dma((8 * steps,)),

time: 190 us -> 185 us (0.974)
  Pallas kernels: 189 us -> 183 us
    pallas_call x1, Pallas kernels: 189 us -> 183 us  [device_step(): pl.pallas_call(functools.partial(step_kernel, dims), out_shape=jax.ShapeD...]
where the time goes in v5:
time: 185 us
  Pallas kernels  183 us (99%)
    pallas_call x1, Pallas kernels, device_step(): pl.pallas_call(functools.partial(step_kernel, dims), out_shape=jax.ShapeD...  183 us

profile of v5, /device:TPU:97, one launch (start us, length us, event | category | flops | bytes accessed | tf_op | source)
XLA Modules:
  0.0 184.6 jit_solution(16692515328822418491)
XLA Ops:
  0.0 182.9 %step.1 = bf16[128,1024]{1,0:T(8,128)(2,1)} custom-call(bf16[128,1024]{1,0:T(8,128)(2,1)} %hidden_ref.1, bf16[2,16384,128]{2,1,0:T(8,128)(2,1)} %bitcast.3, bf16[2,16384,128]{2,1,0:T(8,128)(2,1)} %bitcast.4, s32[128]{0:T(128)} %len_ref.1, bf16[2,1024,2048]{2,1,0:T(8,128)(2,1)} %wq_hbm.1, bf16[2,1024,128]{2,1,0:T(8,128)(2,1)} %wk_hbm.1, ...), custom_call_target="tpu_custom_call" | custom-call | tf_op jit(solution)/shard_map/step/pallas_call | solution.py:650
  182.9 1.7 copy.15

commit v6 on v5

--- a/solution.py
+++ b/solution.py
@@ -437,11 +437,11 @@
         project(0)
         s0(0)
         lax.fori_loop(blocks, 2 * blocks - 1, block, 0)
+        lax.fori_loop(2 * blocks - 1, 2 * blocks, block, 0)
         s2(0)
-        lax.fori_loop(2 * blocks - 1, 2 * blocks, block, 0)
-        s4(0, 0)
         project(1)
         s0(1)
+        s4(0, 0)
         s3(0)
 
         att_copies(layer)[4].wait()
@@ -566,7 +566,7 @@
                         rbuf[pl.ds(row, WINDOW), :] = out[par * WINDOW:(par + 1) * WINDOW, h * LANES:(h + 1) * LANES]
                 return c2
 
-            lax.fori_loop(0, pools, window, 0, unroll=4)
+            lax.fori_loop(0, pools, window, 0, unroll=8)
             for r, flip in firsts:
                 for h in BOTH:
                     go(first_copy, h, w, r, flip)

time: 185 us -> 184 us (level)
  no operation moved by 1% of the time
where the time goes in v6:
time: 184 us; the launch traced here: 183 us
  Pallas kernels  182 us (99%)
    pallas_call x1, Pallas kernels, device_step(): pl.pallas_call(functools.partial(step_kernel, dims), out_shape=jax.ShapeD...  182 us

profile of v6, /device:TPU:97, one launch (start us, length us, event | category | flops | bytes accessed | tf_op | source)
XLA Modules:
  0.0 183.4 jit_solution(6014410357015047840)
XLA Ops:
  0.0 181.7 %step.1 = bf16[128,1024]{1,0:T(8,128)(2,1)} custom-call(bf16[128,1024]{1,0:T(8,128)(2,1)} %hidden_ref.1, bf16[2,16384,128]{2,1,0:T(8,128)(2,1)} %bitcast.3, bf16[2,16384,128]{2,1,0:T(8,128)(2,1)} %bitcast.4, s32[128]{0:T(128)} %len_ref.1, bf16[2,1024,2048]{2,1,0:T(8,128)(2,1)} %wq_hbm.1, bf16[2,1024,128]{2,1,0:T(8,128)(2,1)} %wk_hbm.1, ...), custom_call_target="tpu_custom_call" | custom-call | tf_op jit(solution)/shard_map/step/pallas_call | solution.py:650
  181.7 1.7 copy.15
